TPU v7x, 128 devices: a whole 4x4x4 slice. The times are simulated.
128 devices in a mesh: blk: 16 (over y_hi, x, core), red: 8 (over y_lo, z).
Axes of the slice: x: 4, y: 4 (y_hi: 2, y_lo: 2; y = y_hi * 2 + y_lo), z: 4, core: 2. Of those that a mesh axis runs over, the one named last changes fastest.
Arguments:
- x_now: bfloat16 [1024, 131072], P('blk', 'red'), may hold values from -6 to 6
- x_prev: float32 [1024, 131072], P('blk', 'red'), may hold values from -6 to 6
- density: float32 [1024, 131072], P('blk', 'red'), may hold values from -6 to 6
- coeffs: float32 [8], replicated, may hold values from -1 to 1
- potential: int32 [64], P('blk'), may hold values from 0 to 7
- h_tiles: bfloat16 [16, 96, 256, 256], P('blk', 'red'), may hold values from -0.1796875 to 0.1796875
- tile_rows: int32 [16, 96], P('blk', 'red'), may hold values from 0 to 31
- tile_cols: int32 [16, 96], P('blk', 'red'), may hold values from 0 to 63, as said below
- tile_counts: int32 [16, 8], P('blk', 'red'), may hold values from 3 to 12, as said below
Outputs:
- x_next: float32 [1024, 131072], P('blk', 'red')
- density_out: float32 [1024, 131072], P('blk', 'red')
Inputs may be any that keep to these rules, and one draw needn't show every extreme that they name: `tile_cols`: block column within the group; the live slots of one panel and group name distinct positions (row, column). `tile_counts`: at most 12 live slots; some panel and group is full in every draw.
All inputs are finite; a program needn't handle non-finite values.
Results may differ from a plain program's by a relative error of at most 0.005.
Values may be sent and summed in bfloat16 or wider, within the bound.
A program may use at most 128 MiB of HBM per device.

v0:
```python
import jax
import jax.numpy as jnp
from jax import lax
from jax.sharding import PartitionSpec as P


def for_sending(x):

    def short(part):
        return part.astype(jnp.bfloat16) if part.dtype == jnp.float32 else part

    return jax.tree.map(short, x)


def from_behind(value, axis, steps):
    count = lax.axis_size(axis)
    pairs = [(source, (source + steps) % count) for source in range(count)]
    return lax.ppermute(value, axis, pairs)


def shards(x_now, x_prev, density, coeffs, potential, h_tiles, tile_rows, tile_cols, tile_counts):
    columns, local_rows = x_now.shape
    blk_count = lax.axis_size("blk")
    red_count = lax.axis_size("red")
    tile_width = h_tiles.shape[-1]
    capacity = h_tiles.shape[1]
    col_blocks = local_rows // tile_width
    row_blocks = local_rows * red_count // tile_width // blk_count
    owned_panels = blk_count // red_count
    x_blocks = x_now.reshape(columns, col_blocks, tile_width)
    anchor = lax.axis_index("blk")
    slot_index = jnp.arange(capacity, dtype=jnp.int32)

    def slot_products(state):
        tile_data, row_ids, col_ids, live_count = state
        picked = jnp.take(x_blocks, col_ids, axis=1)
        product = jnp.einsum("vck,cik->cvi", picked, tile_data, preferred_element_type=jnp.float32)
        is_live = slot_index < live_count
        return (product, row_ids, is_live)

    def packed_rows(state):
        product, row_ids, is_live = slot_products(state)
        same_row = (row_ids[:, None] == row_ids[None, :]) & is_live[:, None] & is_live[None, :]
        before = same_row & (slot_index[None, :] < slot_index[:, None])
        leading = is_live & jnp.logical_not(jnp.any(before, axis=1))
        collect = (same_row & leading[:, None]).astype(jnp.float32)
        summed = jnp.einsum("st,tvi->vsi", collect, product)
        values = summed.reshape(columns, 1, capacity * tile_width).astype(jnp.bfloat16)
        numbers = (
            jnp.where(leading, row_ids, -1)
            .astype(jnp.float32)
            .astype(jnp.bfloat16)
            .reshape(1, capacity)
        )
        return (values, numbers)

    holder = (
        jnp.zeros((columns, blk_count, capacity * tile_width), jnp.bfloat16),
        jnp.full((blk_count, capacity), -1.0, jnp.bfloat16),
    )

    def place(totals, state, panel_index):
        where_at = jnp.asarray(panel_index % blk_count, dtype=jnp.int32)
        values, numbers = packed_rows(state)
        stored = lax.dynamic_update_slice_in_dim(totals[0], values, where_at, 1)
        labels = lax.dynamic_update_slice_in_dim(totals[1], numbers, where_at, 0)
        return (stored, labels)

    start_state = (h_tiles[0], tile_rows[0], tile_cols[0], tile_counts[0, 0])
    totals = holder

    def advance(number, carry):
        state, partial_sums = carry
        partial_sums = place(partial_sums, state, anchor - number)
        state = jax.tree.map(
            lambda part, own: part.astype(own.dtype),
            from_behind(for_sending(state), "blk", 1),
            state,
        )
        return (state, partial_sums)

    last_state, totals = lax.fori_loop(0, blk_count - 1, advance, (start_state, totals))
    totals = place(totals, last_state, anchor - (blk_count - 1))
    stored, labels = totals
    stored = stored.reshape(columns, blk_count, 1, capacity * tile_width)
    labels = labels.reshape(1, blk_count, 1, capacity)
    arrived, arrived_labels = (
        lax.all_to_all(stored, "red", split_axis=1, concat_axis=2, tiled=True),
        lax.all_to_all(labels, "red", split_axis=1, concat_axis=2, tiled=True),
    )
    arrived = arrived.reshape(columns, owned_panels, red_count, capacity, tile_width)
    targets = jnp.arange(row_blocks, dtype=jnp.int32).astype(jnp.float32)
    placing = (
        arrived_labels.reshape(owned_panels, red_count, capacity)[:, :, :, None].astype(jnp.float32)
        == targets[None, None, None, :]
    ).astype(jnp.bfloat16)
    gathered = jnp.einsum("prsq,vprsi->vpqi", placing, arrived, preferred_element_type=jnp.float32)
    product = gathered.reshape(columns, local_rows)
    x_next = 2.0 * product - x_prev
    slabs_here = potential.shape[0]
    slab_width = columns // slabs_here
    picking = (potential[:, None] == jnp.arange(coeffs.shape[0], dtype=jnp.int32)[None, :]).astype(
        jnp.float32
    )
    slab_coef = jnp.sum(picking * coeffs[None, :], axis=1)
    column_coef = jnp.repeat(slab_coef, slab_width)
    density_out = density + column_coef[:, None] * x_next
    return (x_next, density_out)


def solution(mesh):
    in_specs = (
        P("blk", "red"),
        P("blk", "red"),
        P("blk", "red"),
        P(),
        P("blk"),
        P("blk", "red", None, None),
        P("blk", "red"),
        P("blk", "red"),
        P("blk", "red"),
    )
    out_specs = (P("blk", "red"), P("blk", "red"))
    return jax.shard_map(shards, mesh=mesh, in_specs=in_specs, out_specs=out_specs, check_vma=False)
```

profile of v0, /device:TPU:13, one launch (start us, length us, event | category | flops | bytes accessed | tf_op | source)
XLA Modules:
  0.0 523.6 jit_solution(14595473268515517830)
XLA Ops:
  9.6 406.5 %while.27 = (s32[]{:T(128)}, bf16[12,256,256]{2,1,0:T(8,128)(2,1)S(1)}, s32[12]{0:T(128)}, s32[12]{0:T(128)}, s32[]{:T(128)}, /*index=5*/bf16[64,16,3072]{2,0,1:...) while((s32[]{:T(128)}, ...), condition=%wide.region_2.4_spmd.clone.clone, body=%wide.region_0.3_spmd.clone.clone.sunk | while | flops 105581144 | bytes 14948048 | solution.py:82
  25.9 7.9 %collective-permute-done = bf16[12,256,256]{2,1,0:T(8,128)(2,1)S(1)} collective-permute-done((bf16[12,256,256]{2,1,0:T(8,128)(2,1)S(1)}, bf16[12,256,256]{2,1,0:T(8,128)(2,1)S(1)}, u32[]{:S(2)}, u32[]{:S(2)}) %collective-permute-start) | collective-permute-done | bytes 1572896 | tf_op jit(solution)/shard_map/while/body/eval_jaxpr/ppermute | solution.py:18
  38.8 5.9 %collective-permute-start.3 = (s32[]{:T(128)}, s32[]{:T(128)}, u32[]{:S(2)}, u32[]{:S(2)}) collective-permute-start(s32[]{:T(128)} %copy.88), channel_id=1, source_target_pairs={{0,8},{8,16},{16,24},{24,32},{32,40},{40,48},{48,56},{56,64},{64,7... | collective-permute-start | bytes 20 | tf_op jit(solution)/shard_map/while/body/eval_jaxpr/ppermute | solution.py:18
  54.7 7.9 %collective-permute-done = bf16[12,256,256]{2,1,0:T(8,128)(2,1)S(1)} collective-permute-done((bf16[12,256,256]{2,1,0:T(8,128)(2,1)S(1)}, bf16[12,256,256]{2,1,0:T(8,128)(2,1)S(1)}, u32[]{:S(2)}, u32[]{:S(2)}) %collective-permute-start) | collective-permute-done | bytes 1572896 | tf_op jit(solution)/shard_map/while/body/eval_jaxpr/ppermute | solution.py:18
  67.5 4.3 collective-permute-start.3
  81.8 7.9 %collective-permute-done = bf16[12,256,256]{2,1,0:T(8,128)(2,1)S(1)} collective-permute-done((bf16[12,256,256]{2,1,0:T(8,128)(2,1)S(1)}, bf16[12,256,256]{2,1,0:T(8,128)(2,1)S(1)}, u32[]{:S(2)}, u32[]{:S(2)}) %collective-permute-start) | collective-permute-done | bytes 1572896 | tf_op jit(solution)/shard_map/while/body/eval_jaxpr/ppermute | solution.py:18
  109.0 7.9 %collective-permute-done = bf16[12,256,256]{2,1,0:T(8,128)(2,1)S(1)} collective-permute-done((bf16[12,256,256]{2,1,0:T(8,128)(2,1)S(1)}, bf16[12,256,256]{2,1,0:T(8,128)(2,1)S(1)}, u32[]{:S(2)}, u32[]{:S(2)}) %collective-permute-start) | collective-permute-done | bytes 1572896 | tf_op jit(solution)/shard_map/while/body/eval_jaxpr/ppermute | solution.py:18
  121.8 4.3 collective-permute-start.3
  136.1 7.9 %collective-permute-done = bf16[12,256,256]{2,1,0:T(8,128)(2,1)S(1)} collective-permute-done((bf16[12,256,256]{2,1,0:T(8,128)(2,1)S(1)}, bf16[12,256,256]{2,1,0:T(8,128)(2,1)S(1)}, u32[]{:S(2)}, u32[]{:S(2)}) %collective-permute-start) | collective-permute-done | bytes 1572896 | tf_op jit(solution)/shard_map/while/body/eval_jaxpr/ppermute | solution.py:18
  163.2 7.9 %collective-permute-done = bf16[12,256,256]{2,1,0:T(8,128)(2,1)S(1)} collective-permute-done((bf16[12,256,256]{2,1,0:T(8,128)(2,1)S(1)}, bf16[12,256,256]{2,1,0:T(8,128)(2,1)S(1)}, u32[]{:S(2)}, u32[]{:S(2)}) %collective-permute-start) | collective-permute-done | bytes 1572896 | tf_op jit(solution)/shard_map/while/body/eval_jaxpr/ppermute | solution.py:18
  176.1 4.3 collective-permute-start.3
  190.4 7.9 %collective-permute-done = bf16[12,256,256]{2,1,0:T(8,128)(2,1)S(1)} collective-permute-done((bf16[12,256,256]{2,1,0:T(8,128)(2,1)S(1)}, bf16[12,256,256]{2,1,0:T(8,128)(2,1)S(1)}, u32[]{:S(2)}, u32[]{:S(2)}) %collective-permute-start) | collective-permute-done | bytes 1572896 | tf_op jit(solution)/shard_map/while/body/eval_jaxpr/ppermute | solution.py:18
  217.6 7.9 %collective-permute-done = bf16[12,256,256]{2,1,0:T(8,128)(2,1)S(1)} collective-permute-done((bf16[12,256,256]{2,1,0:T(8,128)(2,1)S(1)}, bf16[12,256,256]{2,1,0:T(8,128)(2,1)S(1)}, u32[]{:S(2)}, u32[]{:S(2)}) %collective-permute-start) | collective-permute-done | bytes 1572896 | tf_op jit(solution)/shard_map/while/body/eval_jaxpr/ppermute | solution.py:18
  244.7 7.9 %collective-permute-done = bf16[12,256,256]{2,1,0:T(8,128)(2,1)S(1)} collective-permute-done((bf16[12,256,256]{2,1,0:T(8,128)(2,1)S(1)}, bf16[12,256,256]{2,1,0:T(8,128)(2,1)S(1)}, u32[]{:S(2)}, u32[]{:S(2)}) %collective-permute-start) | collective-permute-done | bytes 1572896 | tf_op jit(solution)/shard_map/while/body/eval_jaxpr/ppermute | solution.py:18
  271.9 7.9 %collective-permute-done = bf16[12,256,256]{2,1,0:T(8,128)(2,1)S(1)} collective-permute-done((bf16[12,256,256]{2,1,0:T(8,128)(2,1)S(1)}, bf16[12,256,256]{2,1,0:T(8,128)(2,1)S(1)}, u32[]{:S(2)}, u32[]{:S(2)}) %collective-permute-start) | collective-permute-done | bytes 1572896 | tf_op jit(solution)/shard_map/while/body/eval_jaxpr/ppermute | solution.py:18
  299.0 7.9 %collective-permute-done = bf16[12,256,256]{2,1,0:T(8,128)(2,1)S(1)} collective-permute-done((bf16[12,256,256]{2,1,0:T(8,128)(2,1)S(1)}, bf16[12,256,256]{2,1,0:T(8,128)(2,1)S(1)}, u32[]{:S(2)}, u32[]{:S(2)}) %collective-permute-start) | collective-permute-done | bytes 1572896 | tf_op jit(solution)/shard_map/while/body/eval_jaxpr/ppermute | solution.py:18
  326.1 7.9 %collective-permute-done = bf16[12,256,256]{2,1,0:T(8,128)(2,1)S(1)} collective-permute-done((bf16[12,256,256]{2,1,0:T(8,128)(2,1)S(1)}, bf16[12,256,256]{2,1,0:T(8,128)(2,1)S(1)}, u32[]{:S(2)}, u32[]{:S(2)}) %collective-permute-start) | collective-permute-done | bytes 1572896 | tf_op jit(solution)/shard_map/while/body/eval_jaxpr/ppermute | solution.py:18
  353.3 7.9 %collective-permute-done = bf16[12,256,256]{2,1,0:T(8,128)(2,1)S(1)} collective-permute-done((bf16[12,256,256]{2,1,0:T(8,128)(2,1)S(1)}, bf16[12,256,256]{2,1,0:T(8,128)(2,1)S(1)}, u32[]{:S(2)}, u32[]{:S(2)}) %collective-permute-start) | collective-permute-done | bytes 1572896 | tf_op jit(solution)/shard_map/while/body/eval_jaxpr/ppermute | solution.py:18
  380.4 7.9 %collective-permute-done = bf16[12,256,256]{2,1,0:T(8,128)(2,1)S(1)} collective-permute-done((bf16[12,256,256]{2,1,0:T(8,128)(2,1)S(1)}, bf16[12,256,256]{2,1,0:T(8,128)(2,1)S(1)}, u32[]{:S(2)}, u32[]{:S(2)}) %collective-permute-start) | collective-permute-done | bytes 1572896 | tf_op jit(solution)/shard_map/while/body/eval_jaxpr/ppermute | solution.py:18
  407.5 7.9 %collective-permute-done = bf16[12,256,256]{2,1,0:T(8,128)(2,1)S(1)} collective-permute-done((bf16[12,256,256]{2,1,0:T(8,128)(2,1)S(1)}, bf16[12,256,256]{2,1,0:T(8,128)(2,1)S(1)}, u32[]{:S(2)}, u32[]{:S(2)}) %collective-permute-start) | collective-permute-done | bytes 1572896 | tf_op jit(solution)/shard_map/while/body/eval_jaxpr/ppermute | solution.py:18
  420.3 6.2 %all-to-all-start.1 = ((bf16[1,16,1,12]{3,2,0,1:T(2,128)(2,1)}), bf16[1,16,1,12]{3,2,0,1:T(2,128)(2,1)S(1)}, u32[]{:S(2)}, u32[]{:S(2)}) async-start(bf16[1,16,1,12]{3,2,0,1:T(2,128)(2,1)} %copy.55), calls=%async_computation.1 | async-start | bytes 16384 | tf_op jit(solution)/shard_map/all_to_all | solution.py:89
  432.1 5.3 %all-to-all-start = ((bf16[64,16,1,3072]{3,0,2,1:T(8,128)(2,1)}), bf16[64,16,1,3072]{3,0,2,1:T(8,128)(2,1)}, u32[]{:S(2)}, u32[]{:S(2)}) async-start(bf16[64,16,1,3072]{3,0,2,1:T(8,128)(2,1)} %constant_dynamic-update-slice_fusion.1), calls=%async_computation | async-start | bytes 12582912 | tf_op jit(solution)/shard_map/all_to_all | solution.py:88
  437.8 70.5 %all-to-all-done = bf16[64,16,1,3072]{3,0,2,1:T(8,128)(2,1)} async-done(((bf16[64,16,1,3072]{3,0,2,1:T(8,128)(2,1)}), bf16[64,16,1,3072]{3,0,2,1:T(8,128)(2,1)}, u32[]{:S(2)}, u32[]{:S(2)}) %all-to-all-start) | async-done | bytes 6291488 | tf_op jit(solution)/shard_map/all_to_all | solution.py:88
  508.3 6.2 %copy.53 = bf16[64,2,8,1,3072]{4,2,1,0,3:T(8,128)(2,1)S(1)} copy(bf16[64,2,8,1,3072]{4,0,1,2,3:T(8,128)(2,1)} %bitcast.9) | data formatting | bytes 12582912 | tf_op jit(solution)/shard_map/all_to_all | solution.py:88
  (381 shorter events, 286.1 us)
Async XLA Ops:
  16.1 17.7 %collective-permute-start = (bf16[12,256,256]{2,1,0:T(8,128)(2,1)S(1)}, bf16[12,256,256]{2,1,0:T(8,128)(2,1)S(1)}, u32[]{:S(2)}, u32[]{:S(2)}) collective-permute-start(bf16[12,256,256]{2,1,0:T(8,128)(2,1)S(1)} %copy.85), channel_id=1, source_target_pairs={{0,8},{8,16},{16,24},{24,32},{32,40},{40,48},{48,56},{56,64},{64,7... | collective-permute-start | bytes 4718600 | tf_op jit(solution)/shard_map/while/body/eval_jaxpr/ppermute | solution.py:18
  35.1 19.5 %collective-permute-start.1 = (s32[12]{0:T(128)S(1)}, s32[12]{0:T(128)}, u32[]{:S(2)}, u32[]{:S(2)}) collective-permute-start(s32[12]{0:T(128)S(1)} %copy.86), channel_id=1, source_target_pairs={{0,8},{8,16},{16,24},{24,32},{32,40},{40,48},{48,56},{56,64},{64,7... | collective-permute-start | bytes 152 | tf_op jit(solution)/shard_map/while/body/eval_jaxpr/ppermute | solution.py:18
  44.9 17.7 %collective-permute-start = (bf16[12,256,256]{2,1,0:T(8,128)(2,1)S(1)}, bf16[12,256,256]{2,1,0:T(8,128)(2,1)S(1)}, u32[]{:S(2)}, u32[]{:S(2)}) collective-permute-start(bf16[12,256,256]{2,1,0:T(8,128)(2,1)S(1)} %copy.85), channel_id=1, source_target_pairs={{0,8},{8,16},{16,24},{24,32},{32,40},{40,48},{48,56},{56,64},{64,7... | collective-permute-start | bytes 4718600 | tf_op jit(solution)/shard_map/while/body/eval_jaxpr/ppermute | solution.py:18
  63.9 17.9 %collective-permute-start.1 = (s32[12]{0:T(128)S(1)}, s32[12]{0:T(128)}, u32[]{:S(2)}, u32[]{:S(2)}) collective-permute-start(s32[12]{0:T(128)S(1)} %copy.86), channel_id=1, source_target_pairs={{0,8},{8,16},{16,24},{24,32},{32,40},{40,48},{48,56},{56,64},{64,7... | collective-permute-start | bytes 152 | tf_op jit(solution)/shard_map/while/body/eval_jaxpr/ppermute | solution.py:18
  72.0 17.7 %collective-permute-start = (bf16[12,256,256]{2,1,0:T(8,128)(2,1)S(1)}, bf16[12,256,256]{2,1,0:T(8,128)(2,1)S(1)}, u32[]{:S(2)}, u32[]{:S(2)}) collective-permute-start(bf16[12,256,256]{2,1,0:T(8,128)(2,1)S(1)} %copy.85), channel_id=1, source_target_pairs={{0,8},{8,16},{16,24},{24,32},{32,40},{40,48},{48,56},{56,64},{64,7... | collective-permute-start | bytes 4718600 | tf_op jit(solution)/shard_map/while/body/eval_jaxpr/ppermute | solution.py:18
  91.0 17.9 %collective-permute-start.1 = (s32[12]{0:T(128)S(1)}, s32[12]{0:T(128)}, u32[]{:S(2)}, u32[]{:S(2)}) collective-permute-start(s32[12]{0:T(128)S(1)} %copy.86), channel_id=1, source_target_pairs={{0,8},{8,16},{16,24},{24,32},{32,40},{40,48},{48,56},{56,64},{64,7... | collective-permute-start | bytes 152 | tf_op jit(solution)/shard_map/while/body/eval_jaxpr/ppermute | solution.py:18
  99.1 17.7 %collective-permute-start = (bf16[12,256,256]{2,1,0:T(8,128)(2,1)S(1)}, bf16[12,256,256]{2,1,0:T(8,128)(2,1)S(1)}, u32[]{:S(2)}, u32[]{:S(2)}) collective-permute-start(bf16[12,256,256]{2,1,0:T(8,128)(2,1)S(1)} %copy.85), channel_id=1, source_target_pairs={{0,8},{8,16},{16,24},{24,32},{32,40},{40,48},{48,56},{56,64},{64,7... | collective-permute-start | bytes 4718600 | tf_op jit(solution)/shard_map/while/body/eval_jaxpr/ppermute | solution.py:18
  118.2 17.9 %collective-permute-start.1 = (s32[12]{0:T(128)S(1)}, s32[12]{0:T(128)}, u32[]{:S(2)}, u32[]{:S(2)}) collective-permute-start(s32[12]{0:T(128)S(1)} %copy.86), channel_id=1, source_target_pairs={{0,8},{8,16},{16,24},{24,32},{32,40},{40,48},{48,56},{56,64},{64,7... | collective-permute-start | bytes 152 | tf_op jit(solution)/shard_map/while/body/eval_jaxpr/ppermute | solution.py:18
  145.3 17.9 %collective-permute-start.1 = (s32[12]{0:T(128)S(1)}, s32[12]{0:T(128)}, u32[]{:S(2)}, u32[]{:S(2)}) collective-permute-start(s32[12]{0:T(128)S(1)} %copy.86), channel_id=1, source_target_pairs={{0,8},{8,16},{16,24},{24,32},{32,40},{40,48},{48,56},{56,64},{64,7... | collective-permute-start | bytes 152 | tf_op jit(solution)/shard_map/while/body/eval_jaxpr/ppermute | solution.py:18
  153.4 17.7 %collective-permute-start = (bf16[12,256,256]{2,1,0:T(8,128)(2,1)S(1)}, bf16[12,256,256]{2,1,0:T(8,128)(2,1)S(1)}, u32[]{:S(2)}, u32[]{:S(2)}) collective-permute-start(bf16[12,256,256]{2,1,0:T(8,128)(2,1)S(1)} %copy.85), channel_id=1, source_target_pairs={{0,8},{8,16},{16,24},{24,32},{32,40},{40,48},{48,56},{56,64},{64,7... | collective-permute-start | bytes 4718600 | tf_op jit(solution)/shard_map/while/body/eval_jaxpr/ppermute | solution.py:18
  172.5 17.9 %collective-permute-start.1 = (s32[12]{0:T(128)S(1)}, s32[12]{0:T(128)}, u32[]{:S(2)}, u32[]{:S(2)}) collective-permute-start(s32[12]{0:T(128)S(1)} %copy.86), channel_id=1, source_target_pairs={{0,8},{8,16},{16,24},{24,32},{32,40},{40,48},{48,56},{56,64},{64,7... | collective-permute-start | bytes 152 | tf_op jit(solution)/shard_map/while/body/eval_jaxpr/ppermute | solution.py:18
  199.6 17.9 %collective-permute-start.1 = (s32[12]{0:T(128)S(1)}, s32[12]{0:T(128)}, u32[]{:S(2)}, u32[]{:S(2)}) collective-permute-start(s32[12]{0:T(128)S(1)} %copy.86), channel_id=1, source_target_pairs={{0,8},{8,16},{16,24},{24,32},{32,40},{40,48},{48,56},{56,64},{64,7... | collective-permute-start | bytes 152 | tf_op jit(solution)/shard_map/while/body/eval_jaxpr/ppermute | solution.py:18
  207.7 17.7 %collective-permute-start = (bf16[12,256,256]{2,1,0:T(8,128)(2,1)S(1)}, bf16[12,256,256]{2,1,0:T(8,128)(2,1)S(1)}, u32[]{:S(2)}, u32[]{:S(2)}) collective-permute-start(bf16[12,256,256]{2,1,0:T(8,128)(2,1)S(1)} %copy.85), channel_id=1, source_target_pairs={{0,8},{8,16},{16,24},{24,32},{32,40},{40,48},{48,56},{56,64},{64,7... | collective-permute-start | bytes 4718600 | tf_op jit(solution)/shard_map/while/body/eval_jaxpr/ppermute | solution.py:18
  226.8 18.0 %collective-permute-start.1 = (s32[12]{0:T(128)S(1)}, s32[12]{0:T(128)}, u32[]{:S(2)}, u32[]{:S(2)}) collective-permute-start(s32[12]{0:T(128)S(1)} %copy.86), channel_id=1, source_target_pairs={{0,8},{8,16},{16,24},{24,32},{32,40},{40,48},{48,56},{56,64},{64,7... | collective-permute-start | bytes 152 | tf_op jit(solution)/shard_map/while/body/eval_jaxpr/ppermute | solution.py:18
  253.9 18.0 %collective-permute-start.1 = (s32[12]{0:T(128)S(1)}, s32[12]{0:T(128)}, u32[]{:S(2)}, u32[]{:S(2)}) collective-permute-start(s32[12]{0:T(128)S(1)} %copy.86), channel_id=1, source_target_pairs={{0,8},{8,16},{16,24},{24,32},{32,40},{40,48},{48,56},{56,64},{64,7... | collective-permute-start | bytes 152 | tf_op jit(solution)/shard_map/while/body/eval_jaxpr/ppermute | solution.py:18
  262.0 17.7 %collective-permute-start = (bf16[12,256,256]{2,1,0:T(8,128)(2,1)S(1)}, bf16[12,256,256]{2,1,0:T(8,128)(2,1)S(1)}, u32[]{:S(2)}, u32[]{:S(2)}) collective-permute-start(bf16[12,256,256]{2,1,0:T(8,128)(2,1)S(1)} %copy.85), channel_id=1, source_target_pairs={{0,8},{8,16},{16,24},{24,32},{32,40},{40,48},{48,56},{56,64},{64,7... | collective-permute-start | bytes 4718600 | tf_op jit(solution)/shard_map/while/body/eval_jaxpr/ppermute | solution.py:18
  281.0 18.0 %collective-permute-start.1 = (s32[12]{0:T(128)S(1)}, s32[12]{0:T(128)}, u32[]{:S(2)}, u32[]{:S(2)}) collective-permute-start(s32[12]{0:T(128)S(1)} %copy.86), channel_id=1, source_target_pairs={{0,8},{8,16},{16,24},{24,32},{32,40},{40,48},{48,56},{56,64},{64,7... | collective-permute-start | bytes 152 | tf_op jit(solution)/shard_map/while/body/eval_jaxpr/ppermute | solution.py:18
  308.2 17.9 %collective-permute-start.1 = (s32[12]{0:T(128)S(1)}, s32[12]{0:T(128)}, u32[]{:S(2)}, u32[]{:S(2)}) collective-permute-start(s32[12]{0:T(128)S(1)} %copy.86), channel_id=1, source_target_pairs={{0,8},{8,16},{16,24},{24,32},{32,40},{40,48},{48,56},{56,64},{64,7... | collective-permute-start | bytes 152 | tf_op jit(solution)/shard_map/while/body/eval_jaxpr/ppermute | solution.py:18
  316.3 17.7 %collective-permute-start = (bf16[12,256,256]{2,1,0:T(8,128)(2,1)S(1)}, bf16[12,256,256]{2,1,0:T(8,128)(2,1)S(1)}, u32[]{:S(2)}, u32[]{:S(2)}) collective-permute-start(bf16[12,256,256]{2,1,0:T(8,128)(2,1)S(1)} %copy.85), channel_id=1, source_target_pairs={{0,8},{8,16},{16,24},{24,32},{32,40},{40,48},{48,56},{56,64},{64,7... | collective-permute-start | bytes 4718600 | tf_op jit(solution)/shard_map/while/body/eval_jaxpr/ppermute | solution.py:18
  335.3 18.0 %collective-permute-start.1 = (s32[12]{0:T(128)S(1)}, s32[12]{0:T(128)}, u32[]{:S(2)}, u32[]{:S(2)}) collective-permute-start(s32[12]{0:T(128)S(1)} %copy.86), channel_id=1, source_target_pairs={{0,8},{8,16},{16,24},{24,32},{32,40},{40,48},{48,56},{56,64},{64,7... | collective-permute-start | bytes 152 | tf_op jit(solution)/shard_map/while/body/eval_jaxpr/ppermute | solution.py:18
  362.5 17.9 %collective-permute-start.1 = (s32[12]{0:T(128)S(1)}, s32[12]{0:T(128)}, u32[]{:S(2)}, u32[]{:S(2)}) collective-permute-start(s32[12]{0:T(128)S(1)} %copy.86), channel_id=1, source_target_pairs={{0,8},{8,16},{16,24},{24,32},{32,40},{40,48},{48,56},{56,64},{64,7... | collective-permute-start | bytes 152 | tf_op jit(solution)/shard_map/while/body/eval_jaxpr/ppermute | solution.py:18
  370.6 17.7 %collective-permute-start = (bf16[12,256,256]{2,1,0:T(8,128)(2,1)S(1)}, bf16[12,256,256]{2,1,0:T(8,128)(2,1)S(1)}, u32[]{:S(2)}, u32[]{:S(2)}) collective-permute-start(bf16[12,256,256]{2,1,0:T(8,128)(2,1)S(1)} %copy.85), channel_id=1, source_target_pairs={{0,8},{8,16},{16,24},{24,32},{32,40},{40,48},{48,56},{56,64},{64,7... | collective-permute-start | bytes 4718600 | tf_op jit(solution)/shard_map/while/body/eval_jaxpr/ppermute | solution.py:18
  389.6 17.9 %collective-permute-start.1 = (s32[12]{0:T(128)S(1)}, s32[12]{0:T(128)}, u32[]{:S(2)}, u32[]{:S(2)}) collective-permute-start(s32[12]{0:T(128)S(1)} %copy.86), channel_id=1, source_target_pairs={{0,8},{8,16},{16,24},{24,32},{32,40},{40,48},{48,56},{56,64},{64,7... | collective-permute-start | bytes 152 | tf_op jit(solution)/shard_map/while/body/eval_jaxpr/ppermute | solution.py:18
  432.1 76.2 %all-to-all-start = ((bf16[64,16,1,3072]{3,0,2,1:T(8,128)(2,1)}), bf16[64,16,1,3072]{3,0,2,1:T(8,128)(2,1)}, u32[]{:S(2)}, u32[]{:S(2)}) async-start(bf16[64,16,1,3072]{3,0,2,1:T(8,128)(2,1)} %constant_dynamic-update-slice_fusion.1), calls=%async_computation | async-start | bytes 12582912 | tf_op jit(solution)/shard_map/all_to_all | solution.py:88
  (59 other events, 643.5 us)
where the time goes:
time: 527 us; the launch traced here: 524 us
  waiting for transfers between devices  189 us (36%)
  local copies, waits for them, and re-layouts  137 us (26%)
  starting transfers between devices  118 us (22%)
  other arithmetic  37.9 us (7%)
  matrix products  29.6 us (6%)
  loops' own time  10.4 us (2%)
    ppermute x60, waiting for transfers between devices, from_behind(): return lax.ppermute(value, axis, pairs)  118 us
    ppermute x60, starting transfers between devices, from_behind(): return lax.ppermute(value, axis, pairs)  107 us
    all_to_all x1, waiting for transfers between devices, shards(): lax.all_to_all(stored, 'red', split_axis=1, concat_axis=2, tiled=True)  70.5 us
    gather x16, local copies, waits for them, and re-layouts, slot_products(): picked = jnp.take(x_blocks, col_ids, axis=1)  34.6 us
    while x75, local copies, waits for them, and re-layouts  29.4 us
    dynamic_update_slice x17, local copies, waits for them, and re-layouts, place(): labels = lax.dynamic_update_slice_in_dim(totals[1], numbers, where_at, 0)  21.9 us
    convert_element_type x16, local copies, waits for them, and re-layouts, packed_rows(): summed.reshape(columns, 1, capacity * tile_width).astype(jnp.bfloat16)  20.1 us
    dot_general x16, matrix products, packed_rows(): summed = jnp.einsum('st,tvi->vsi', collect, product)  18.9 us
  transfers between devices with their start and end apart: 62, of which 16 were waited for; matrix products, arithmetic and copies ran while one was open for 32% of the time, Pallas kernels for 0%

commit v1 on v0

v1 whole, which is shorter than its diff:
```python
import functools

import jax
import jax.numpy as jnp
from jax import lax
from jax.experimental import pallas as pl
from jax.experimental.pallas import tpu as pltpu
from jax.sharding import PartitionSpec as P

MESH = pl.DeviceIdType.MESH
NX = 4
LAG = 3
CHUNK = 3


def place():
    blk = lax.axis_index("blk")
    red = lax.axis_index("red")
    core = lax.rem(blk, 2)
    x = lax.rem(blk // 2, NX)
    yh = blk // (2 * NX)
    yl = red // NX
    z = lax.rem(red, NX)
    return x, yh, yl, z, core


def device(x, y, z, core):
    return ((y // 2) * (2 * NX) + x * 2 + core, lax.rem(y, 2) * NX + z)


def wrap(value):
    return lax.rem(value + 2 * NX, NX)


def exchange(cap, slab, bs, x_ref, h_ref, m_ref, out_ref, mout_ref, near_x, far_x, hb, cb, mbuf, msm,
             xs_sem, xr_sem, xl_sem, ys_sem, yr_sem, rs_sem, rr_sem, fs_sem, cs_sem, cr_sem,
             ms_sem, mr_sem, ns_sem, nr_sem, sm_sem):
    x, yh, yl, z, core = place()
    y = yh * 2 + yl
    other = 1 - core
    total = 2 * cap
    outer = jnp.logical_or(y == 0, y == 3)
    inner = jnp.logical_not(outer)

    def remote(src, dst, send, recv, to):
        return pltpu.make_async_remote_copy(
            src_ref=src, dst_ref=dst, send_sem=send, recv_sem=recv, device_id=to, device_id_type=MESH
        )

    here = (lax.axis_index("blk"), lax.axis_index("red"))
    sibling = device(x, y, z, other)
    x_up = device(wrap(x + 1), y, z, core)
    x_down = device(wrap(x - 1), y, z, core)
    y_pair = yh * 2 + (1 - yl)
    pair = device(x, y_pair, z, core)

    barrier = pltpu.get_barrier_semaphore()
    greeted = 0
    for dx in range(NX):
        for dy in range(NX):
            if dx or dy:
                pl.semaphore_signal(barrier, inc=1, device_id=device(wrap(x + dx), wrap(y + dy), z, core),
                                    device_id_type=MESH)
                greeted += 1
    for dz in range(NX):
        for dc in range(2):
            if dz or dc:
                to = device(x, y, wrap(z + dz), other if dc else core)
                pl.semaphore_signal(barrier, inc=1, device_id=to, device_id_type=MESH)
                greeted += 1
    blocks = near_x.shape[1]

    def load_x(b, carry):
        columns = pl.ds(pl.multiple_of(b * bs, bs), bs)
        pltpu.make_async_copy(x_ref.at[:, columns], near_x.at[core, b], xl_sem).start()
        return carry

    lax.fori_loop(0, blocks, load_x, 0)
    own_x = pltpu.make_async_copy(far_x.at[core], near_x.at[core], xl_sem)

    @pl.when(outer)
    def _():
        def load(t, carry):
            pltpu.make_async_copy(h_ref.at[0, t], hb.at[0, 0, t], yr_sem.at[0, t]).start()
            return carry
        lax.fori_loop(0, cap, load, 0)

    pl.semaphore_wait(barrier, greeted)

    group = jnp.where(outer, 0, 1)
    for d in range(NX):
        for half in range(2):
            y_to = half * 2 + yh
            to = device(wrap(x - d), y_to, z, core)
            if d == 0:
                @pl.when(y_to != y)
                def _(to=to, d=d, half=half):
                    remote(m_ref, mbuf.at[group, d], ms_sem.at[half, d], mr_sem.at[group, d], to).start()

                @pl.when(y_to == y)
                def _(d=d):
                    pltpu.make_async_copy(m_ref, mbuf.at[group, d], mr_sem.at[group, d]).start()
            else:
                remote(m_ref, mbuf.at[group, d], ms_sem.at[half, d], mr_sem.at[group, d], to).start()

    own_x.wait()
    to_sibling = remote(near_x.at[core], near_x.at[core], xs_sem.at[0], xr_sem.at[0], sibling)
    to_sibling.start()
    to_pair = remote(near_x.at[core], far_x.at[core], xs_sem.at[1], xr_sem.at[1], pair)
    forward_x = remote(far_x.at[core], far_x.at[core], xs_sem.at[2], xr_sem.at[2], sibling)
    far = device(x, wrap(y + 2), z, core)
    near = (device(x, y_pair, z, core), device(x, wrap(y_pair + 2), z, core))

    @pl.when(outer)
    def _():
        def send(t, carry):
            remote(h_ref.at[0, t], hb.at[0, 0, t], ys_sem.at[0], yr_sem.at[0, t], far).start()
            return carry
        lax.fori_loop(0, cap, send, 0)
        to_pair.start()

    @pl.when(inner)
    def _():
        to_pair.start()

        def send(t, carry):
            for n in range(2):
                remote(h_ref.at[0, t], hb.at[1, 0, t], ys_sem.at[n], yr_sem.at[1, t], near[n]).start()
            return carry
        lax.fori_loop(0, cap, send, 0)

    for s in range(2):
        for d in range(NX):
            pltpu.make_async_copy(m_ref, mbuf.at[s, d], mr_sem.at[s, d]).wait()
    into_smem = pltpu.make_async_copy(mbuf, msm, sm_sem)
    into_smem.start()
    to_sibling.wait_recv()
    into_smem.wait()

    def side(s):
        return jnp.where(s == 0, yl, 1 - yl)

    for s in range(2):
        for dz in range(NX):
            z_to = wrap(z + dz)
            d = wrap(z_to - x)
            for dc in range(2):
                if dz or dc:
                    to = device(x, y, z_to, other if dc else core)
                    remote(mbuf.at[s, d], mout_ref.at[core, side(s), z], ns_sem.at[s, dz, dc],
                           nr_sem.at[core, side(s), z], to).start()
                else:
                    pltpu.make_async_copy(mbuf.at[s, d], mout_ref.at[core, side(s), z],
                                          nr_sem.at[core, side(s), z]).start()

    def send_chunk(q):
        s = q // (cap // CHUNK)
        first = lax.rem(q, cap // CHUNK) * CHUNK
        slots = pl.ds(first, CHUNK)
        for dz in range(NX):
            z_to = wrap(z + dz)
            d = wrap(z_to - x)
            for dc in range(2):
                c_to = other if dc else core
                src = cb.at[s, d, c_to, slots]
                dst = out_ref.at[core, side(s), z, slots]
                arrived = cr_sem.at[core, side(s), z]
                if dz or dc:
                    remote(src, dst, cs_sem.at[s, dz, dc], arrived, device(x, y, z_to, c_to)).start()
                else:
                    pltpu.make_async_copy(src, dst, arrived).start()

    def multiply(s, t, carry):
        k = s * cap + t
        held_x = far_x if s else near_x

        @pl.when(jnp.logical_and(lax.rem(k, CHUNK) == 0, k > 0))
        def _():
            send_chunk(k // CHUNK - 1)

        if s:
            @pl.when(t == 0)
            def _():
                to_pair.wait_recv()
                forward_x.start()
                forward_x.wait_recv()

        pltpu.make_async_copy(h_ref.at[0, 0], hb.at[s, 2, t], rr_sem.at[2, k]).wait()
        for d in range(NX):
            column = msm[s, d, 0, t]
            picked = jnp.concatenate([held_x[0, column], held_x[1, column]], axis=0)
            product = lax.dot_general(
                picked, hb[s, d, t], (((1,), (1,)), ((), ())), preferred_element_type=jnp.float32
            ).astype(jnp.bfloat16)
            cb[s, d, 0, t] = product[:slab]
            cb[s, d, 1, t] = product[slab:]
        return carry

    def reach(i):
        free = i - 2 * LAG + 1
        held = jnp.where(jnp.logical_and(inner, i < cap + 2 * LAG + 3), jnp.minimum(free, cap), free)
        return jnp.clip(held, 0, total)

    def step(i, carry):
        @pl.when(i < total)
        def _():
            s = i // cap
            t = lax.rem(i, cap)
            pltpu.make_async_copy(h_ref.at[0, 0], hb.at[s, 0, t], yr_sem.at[s, t]).wait()
            mine = hb.at[s, 0, t]
            remote(mine, hb.at[s, 3, t], rs_sem.at[0, s], rr_sem.at[3, i], x_up).start()
            remote(mine, hb.at[s, 1, t], rs_sem.at[1, s], rr_sem.at[1, i], x_down).start()

        @pl.when(jnp.logical_and(i >= LAG, i < total + LAG))
        def _():
            j = i - LAG
            s = j // cap
            t = lax.rem(j, cap)
            for d in (1, 3):
                pltpu.make_async_copy(h_ref.at[0, 0], hb.at[s, d, t], rr_sem.at[d, j]).wait()

            @pl.when(lax.rem(j, 2) == 0)
            def _():
                remote(hb.at[s, 3, t], hb.at[s, 2, t], fs_sem.at[0, s], rr_sem.at[2, j], x_up).start()

            @pl.when(lax.rem(j, 2) == 1)
            def _():
                remote(hb.at[s, 1, t], hb.at[s, 2, t], fs_sem.at[1, s], rr_sem.at[2, j], x_down).start()

        done, until = reach(i - 1), reach(i)
        lax.fori_loop(jnp.minimum(done, cap), jnp.minimum(until, cap), functools.partial(multiply, 0), 0)
        lax.fori_loop(jnp.maximum(done - cap, 0), jnp.maximum(until - cap, 0), functools.partial(multiply, 1), 0)
        return carry

    lax.fori_loop(0, total + 2 * LAG, step, 0)

    to_sibling.wait_send()
    to_pair.wait_send()
    forward_x.wait_send()
    pltpu.make_async_copy(h_ref.at[0], hb.at[0, 0], ys_sem.at[0]).wait()

    @pl.when(inner)
    def _():
        pltpu.make_async_copy(h_ref.at[0], hb.at[0, 0], ys_sem.at[1]).wait()

    send_chunk(jnp.int32(total // CHUNK - 1))
    for way in range(2):
        for s in range(2):
            pltpu.make_async_copy(h_ref.at[0], hb.at[s, 0], rs_sem.at[way, s]).wait()
            pltpu.make_async_copy(h_ref.at[0, pl.ds(0, cap // 2)], hb.at[s, 0, pl.ds(0, cap // 2)],
                                  fs_sem.at[way, s]).wait()
    for half in range(2):
        for d in range(NX):
            if d == 0:
                @pl.when(half * 2 + yh != y)
                def _(half=half, d=d):
                    pltpu.make_async_copy(m_ref, mbuf.at[0, 0], ms_sem.at[half, d]).wait()
            else:
                pltpu.make_async_copy(m_ref, mbuf.at[0, 0], ms_sem.at[half, d]).wait()
    for s in range(2):
        for dz in range(NX):
            for dc in range(2):
                if dz or dc:
                    pltpu.make_async_copy(mbuf.at[0, 0], mout_ref.at[0, 0, 0], ns_sem.at[s, dz, dc]).wait()
                    pltpu.make_async_copy(cb.at[0, 0, 0], out_ref.at[0, 0, 0], cs_sem.at[s, dz, dc]).wait()
    for c in range(2):
        for g in range(2):
            for q in range(NX):
                pltpu.make_async_copy(mbuf.at[0, 0], mout_ref.at[c, g, q], nr_sem.at[c, g, q]).wait()
                pltpu.make_async_copy(cb.at[0, 0, 0], out_ref.at[c, g, q], cr_sem.at[c, g, q]).wait()


def combine(cap, bs, slabs, steps, meta, coeffs, potential, c_ref, prev_ref, dens_ref, next_ref, dout_ref, acc):
    panel = pl.program_id(0)
    part = pl.program_id(1)
    columns = prev_ref.shape[0]
    width = prev_ref.shape[1]

    @pl.when(part == 0)
    def _():
        acc[...] = jnp.zeros_like(acc)
        for g in range(2):
            for q in range(NX):
                for t in range(cap):
                    row = pl.multiple_of(meta[panel, g, q, 1, t] * bs, bs)
                    acc[:, pl.ds(row, bs)] += c_ref[0, g, q, t].astype(jnp.float32)

    height = columns // slabs
    base = pl.multiple_of(part * width, width)
    for s in range(slabs):
        rows = pl.ds(s * height, height)
        value = 2.0 * acc[rows, pl.ds(base, width)] - prev_ref[rows, :]
        next_ref[rows, :] = value
        dout_ref[rows, :] = dens_ref[rows, :] + coeffs[potential[s]] * value


def shards(x_now, x_prev, density, coeffs, potential, h_tiles, tile_rows, tile_cols, tile_counts):
    columns, local_rows = x_now.shape
    cap = h_tiles.shape[1]
    bs = h_tiles.shape[-1]
    slabs = potential.shape[0]
    panel_rows = local_rows // bs // 2
    live = jnp.arange(cap, dtype=jnp.int32)[None, :] < tile_counts
    rows = jnp.where(live, tile_rows, panel_rows)
    lane_pad = ((0, 0), (0, 128 - cap))
    meta = jnp.concatenate([jnp.pad(tile_cols, lane_pad), jnp.pad(rows, lane_pad),
                            jnp.zeros((6, 128), jnp.int32)], axis=0)
    dma = pltpu.SemaphoreType.DMA
    bf16 = jnp.bfloat16
    anywhere = pl.BlockSpec(memory_space=pl.ANY)
    flops = 2 * 8 * cap * 2 * columns * bs * bs
    sums, places = pl.pallas_call(
        functools.partial(exchange, cap, columns, bs),
        out_shape=(
            jax.ShapeDtypeStruct((2, 2, NX, cap, columns, bs), bf16),
            jax.ShapeDtypeStruct((2, 2, NX, 8, 128), jnp.int32),
        ),
        in_specs=[anywhere, anywhere, pl.BlockSpec(memory_space=pltpu.VMEM)],
        out_specs=(anywhere, anywhere),
        scratch_shapes=[
            pltpu.VMEM((2, local_rows // bs, columns, bs), bf16),
            pltpu.VMEM((2, local_rows // bs, columns, bs), bf16),
            pltpu.VMEM((2, NX, cap, bs, bs), bf16),
            pltpu.VMEM((2, NX, 2, cap, columns, bs), bf16),
            pltpu.VMEM((2, NX, 8, 128), jnp.int32),
            pltpu.SMEM((2, NX, 8, 128), jnp.int32),
            dma((3,)), dma((3,)), dma,
            dma((2,)), dma((2, cap)),
            dma((2, 2)), dma((4, 2 * cap)), dma((2, 2)),
            dma((2, NX, 2)), dma((2, 2, NX)),
            dma((2, NX)), dma((2, NX)),
            dma((2, NX, 2)), dma((2, 2, NX)), dma,
        ],
        compiler_params=pltpu.CompilerParams(
            collective_id=0, has_side_effects=True, vmem_limit_bytes=56 * 1024 * 1024
        ),
        cost_estimate=pl.CostEstimate(flops=flops, bytes_accessed=16 * 1024 * 1024, transcendentals=0),
        name="exchange",
    )(x_now, h_tiles, meta)
    parts = 4
    width = local_rows // 2 // parts
    wide = pl.BlockSpec((columns, width), lambda p, i, *_: (0, p * parts + i))
    return tuple(pl.pallas_call(
        functools.partial(combine, cap, bs, slabs, parts),
        out_shape=(
            jax.ShapeDtypeStruct((columns, local_rows), jnp.float32),
            jax.ShapeDtypeStruct((columns, local_rows), jnp.float32),
        ),
        grid_spec=pltpu.PrefetchScalarGridSpec(
            num_scalar_prefetch=3,
            grid=(2, parts),
            in_specs=[
                pl.BlockSpec((1, 2, NX, cap, columns, bs), lambda p, i, *_: (p, 0, 0, 0, 0, 0)),
                wide, wide,
            ],
            out_specs=(wide, wide),
            scratch_shapes=[pltpu.VMEM((columns, (panel_rows + 1) * bs), jnp.float32)],
        ),
        compiler_params=pltpu.CompilerParams(vmem_limit_bytes=48 * 1024 * 1024),
        cost_estimate=pl.CostEstimate(flops=8 * columns * local_rows, bytes_accessed=24 * 1024 * 1024,
                                      transcendentals=0),
        name="combine",
    )(places, coeffs, potential, sums, x_prev, density))


def solution(mesh):
    in_specs = (
        P("blk", "red"),
        P("blk", "red"),
        P("blk", "red"),
        P(),
        P("blk"),
        P("blk", "red", None, None),
        P("blk", "red"),
        P("blk", "red"),
        P("blk", "red"),
    )
    out_specs = (P("blk", "red"), P("blk", "red"))
    return jax.shard_map(shards, mesh=mesh, in_specs=in_specs, out_specs=out_specs, check_vma=False)
```

time: 527 us -> 169 us (0.32)
  waiting for transfers between devices: 189 us -> 0 us
  Pallas kernels: 0 us -> 162 us
  local copies, waits for them, and re-layouts: 137 us -> 0.92 us
  starting transfers between devices: 118 us -> 0 us
  other arithmetic: 37.9 us -> 2.4 us
  matrix products: 29.6 us -> 0 us
  loops' own time: 10.4 us -> 0 us
    pallas_call x0 -> x2, Pallas kernels: none -> 162 us  [the longest x1 148 us: shards(): pl.pallas_call(functools.partial(exchange, cap, columns, bs), out_shape=(...]
    ppermute x60 -> x0, waiting for transfers between devices: 118 us -> none  [from_behind(): return lax.ppermute(value, axis, pairs)]
    ppermute x60 -> x0, starting transfers between devices: 107 us -> none  [from_behind(): return lax.ppermute(value, axis, pairs)]
    all_to_all x2 -> x0, waiting for transfers between devices: 70.5 us -> none  [the longest x1 70.5 us: shards(): lax.all_to_all(stored, 'red', split_axis=1, concat_axis=2, tiled=True)]
    gather x16 -> x0, local copies, waits for them, and re-layouts: 34.6 us -> none  [slot_products(): picked = jnp.take(x_blocks, col_ids, axis=1)]
    dynamic_update_slice x33 -> x0, local copies, waits for them, and re-layouts: 34.4 us -> none  [the longest x17 21.9 us: place(): labels = lax.dynamic_update_slice_in_dim(totals[1], numbers, where_at, 0)]
    dot_general x33 -> x0, matrix products: 29.6 us -> none  [the longest x16 18.9 us: packed_rows(): summed = jnp.einsum('st,tvi->vsi', collect, product)]
    while x75 -> x0, local copies, waits for them, and re-layouts: 29.4 us -> none
  transfers between devices with their start and end apart: 62 -> 0, of which waited for: 16 -> 0; matrix products, arithmetic and copies ran while one was open for 32% -> 0% of each run, Pallas kernels for 0% -> 0%
where the time goes in v1:
time: 169 us; the launch traced here: 167 us
  Pallas kernels  162 us (96%)
  other arithmetic  2.4 us (1%)
    pallas_call x1, Pallas kernels, shards(): pl.pallas_call(functools.partial(exchange, cap, columns, bs), out_shape=(...  148 us
    pallas_call x1, Pallas kernels, shards(): pl.pallas_call(functools.partial(combine, cap, bs, slabs, parts), out_sha...  13.3 us

profile of v1, /device:TPU:13, one launch (start us, length us, event | category | flops | bytes accessed | tf_op | source)
XLA Modules:
  0.0 166.6 jit_solution(16682794004739144516)
XLA Ops:
  0.6 0.0 copy-start.3
  0.6 0.0 copy-start.2
  0.7 0.0 copy-start
  1.5 1.1 compare_select_fusion
  2.5 0.1 pad.11.clone
  2.6 1.3 fusion.m_ref
  3.9 148.5 %exchange.1 = (bf16[2,2,4,12,64,256]{5,4,3,2,1,0:T(8,128)(2,1)}, s32[2,2,4,8,128]{4,3,2,1,0:T(8,128)}) custom-call(bf16[64,16384]{1,0:T(8,128)(2,1)} %x_ref.1, bf16[1,12,256,256]{3,2,1,0:T(8,128)(2,1)} %h_ref.1, s32[8,128]{1,0:T(8,128)} %fusion.m_ref), custom_call_target="tpu_custom_call" | custom-call | flops 1610612736 | bytes 16777216 | tf_op jit(solution)/shard_map/exchange/pallas_call | solution.py:312
  152.4 0.0 copy-done.3
  152.4 0.0 copy-done.2
  152.4 0.0 copy-done
  152.5 0.0 copy-start.1
  152.5 0.8 copy-done.1
  153.3 13.3 %combine.1 = (f32[64,16384]{1,0:T(8,128)}, f32[64,16384]{1,0:T(8,128)}) custom-call(s32[2,2,4,8,128]{4,3,2,1,0:T(8,128)S(1)} %copy-done.1, f32[8]{0:T(128)S(1)} %copy-done.2, s32[4]{0:T(128)S(1)} %copy-done.3, bf16[2,2,4,12,64,256]{5,4,3,2,1,0:T(8,128)(2,1)} %get-tuple-element.5.c_ref, f32[64,16384]{1,0:T(8,128)S(1)} %copy-done, f32[64,16384]{1,0:T(8,128)} %dens_ref.1), custom_call_target="tpu_custom_call" | custom-call | flops 8388608 | bytes 25165824 | tf_op jit(solution)/shard_map/combine/pallas_call | solution.py:343
  (1 shorter events, 0.0 us)
Async XLA Ops:
  0.6 151.8 %copy-start.3 = (s32[4]{0:T(128)S(1)}, s32[4]{0:T(128)}, u32[]{:S(2)}) copy-start(s32[4]{0:T(128)} %potential.1) | copy-start | bytes 52
  0.6 151.8 %copy-start.2 = (f32[8]{0:T(128)S(1)}, f32[8]{0:T(128)}, u32[]{:S(2)}) copy-start(f32[8]{0:T(128)} %coeffs.1) | copy-start | bytes 100
  0.7 151.8 %copy-start = (f32[64,16384]{1,0:T(8,128)S(1)}, f32[64,16384]{1,0:T(8,128)}, u32[]{:S(2)}) copy-start(f32[64,16384]{1,0:T(8,128)} %prev_ref.1) | copy-start | bytes 12582916
  152.5 0.8 copy-start.1

commit v2 on v1

--- a/solution.py
+++ b/solution.py
@@ -9,8 +9,9 @@
 
 MESH = pl.DeviceIdType.MESH
 NX = 4
-LAG = 3
-CHUNK = 3
+LAG = 4
+CHUNK = 1
+HOLD = 12
 
 
 def place():
@@ -32,7 +33,7 @@
     return lax.rem(value + 2 * NX, NX)
 
 
-def exchange(cap, slab, bs, x_ref, h_ref, m_ref, out_ref, mout_ref, near_x, far_x, hb, cb, mbuf, msm,
+def exchange(cap, slab, bs, x_ref, h_ref, cols_ref, rows_ref, count_ref, out_ref, mout_ref, first_x, second_x, hb, cb, m_own, mbuf, msm,
              xs_sem, xr_sem, xl_sem, ys_sem, yr_sem, rs_sem, rr_sem, fs_sem, cs_sem, cr_sem,
              ms_sem, mr_sem, ns_sem, nr_sem, sm_sem):
     x, yh, yl, z, core = place()
@@ -68,15 +69,29 @@
                 to = device(x, y, wrap(z + dz), other if dc else core)
                 pl.semaphore_signal(barrier, inc=1, device_id=to, device_id_type=MESH)
                 greeted += 1
-    blocks = near_x.shape[1]
-
-    def load_x(b, carry):
-        columns = pl.ds(pl.multiple_of(b * bs, bs), bs)
-        pltpu.make_async_copy(x_ref.at[:, columns], near_x.at[core, b], xl_sem).start()
-        return carry
-
-    lax.fori_loop(0, blocks, load_x, 0)
-    own_x = pltpu.make_async_copy(far_x.at[core], near_x.at[core], xl_sem)
+    blocks = first_x.shape[1]
+    m_ref = m_own
+    m_ref[...] = jnp.zeros(m_ref.shape, m_ref.dtype)
+    m_ref[0:1, 0:cap] = cols_ref[...]
+    m_ref[1:2, 0:cap] = rows_ref[...]
+    m_ref[2:3, 0:1] = count_ref[...]
+
+    def load_x(held):
+        def one(b, carry):
+            columns = pl.ds(pl.multiple_of(b * bs, bs), bs)
+            pltpu.make_async_copy(x_ref.at[:, columns], held.at[core, b], xl_sem).start()
+            return carry
+        lax.fori_loop(0, blocks, one, 0)
+
+    @pl.when(outer)
+    def _():
+        load_x(first_x)
+
+    @pl.when(inner)
+    def _():
+        load_x(second_x)
+
+    own_x = pltpu.make_async_copy(second_x.at[core], first_x.at[core], xl_sem)
 
     @pl.when(outer)
     def _():
@@ -87,47 +102,61 @@
 
     pl.semaphore_wait(barrier, greeted)
 
-    group = jnp.where(outer, 0, 1)
     for d in range(NX):
         for half in range(2):
             y_to = half * 2 + yh
+            to_outer = jnp.logical_or(y_to == 0, y_to == 3)
+            phase = jnp.where(to_outer == outer, 0, 1)
             to = device(wrap(x - d), y_to, z, core)
             if d == 0:
                 @pl.when(y_to != y)
-                def _(to=to, d=d, half=half):
-                    remote(m_ref, mbuf.at[group, d], ms_sem.at[half, d], mr_sem.at[group, d], to).start()
+                def _(to=to, d=d, half=half, phase=phase):
+                    remote(m_ref, mbuf.at[phase, d], ms_sem.at[half, d], mr_sem.at[phase, d], to).start()
 
                 @pl.when(y_to == y)
-                def _(d=d):
-                    pltpu.make_async_copy(m_ref, mbuf.at[group, d], mr_sem.at[group, d]).start()
+                def _(d=d, phase=phase):
+                    pltpu.make_async_copy(m_ref, mbuf.at[phase, d], mr_sem.at[phase, d]).start()
             else:
-                remote(m_ref, mbuf.at[group, d], ms_sem.at[half, d], mr_sem.at[group, d], to).start()
+                remote(m_ref, mbuf.at[phase, d], ms_sem.at[half, d], mr_sem.at[phase, d], to).start()
 
     own_x.wait()
-    to_sibling = remote(near_x.at[core], near_x.at[core], xs_sem.at[0], xr_sem.at[0], sibling)
-    to_sibling.start()
-    to_pair = remote(near_x.at[core], far_x.at[core], xs_sem.at[1], xr_sem.at[1], pair)
-    forward_x = remote(far_x.at[core], far_x.at[core], xs_sem.at[2], xr_sem.at[2], sibling)
     far = device(x, wrap(y + 2), z, core)
-    near = (device(x, y_pair, z, core), device(x, wrap(y_pair + 2), z, core))
+    near = (pair, device(x, wrap(y_pair + 2), z, core))
+
+    def x_copies(own, other_x):
+        return (
+            remote(own.at[core], own.at[core], xs_sem.at[0], xr_sem.at[0], sibling),
+            remote(own.at[core], own.at[core], xs_sem.at[1], xr_sem.at[1], pair),
+            remote(other_x.at[core], other_x.at[core], xs_sem.at[2], xr_sem.at[2], sibling),
+        )
+
+    to_sibling, to_pair, forward_x = x_copies(first_x, second_x)
+    to_sibling_in, to_pair_in, forward_x_in = x_copies(second_x, first_x)
 
     @pl.when(outer)
     def _():
+        to_pair.start()
+        to_sibling.start()
+
         def send(t, carry):
-            remote(h_ref.at[0, t], hb.at[0, 0, t], ys_sem.at[0], yr_sem.at[0, t], far).start()
+            remote(h_ref.at[0, t], hb.at[1, 0, t], ys_sem.at[0], yr_sem.at[1, t], far).start()
             return carry
         lax.fori_loop(0, cap, send, 0)
-        to_pair.start()
 
     @pl.when(inner)
     def _():
-        to_pair.start()
+        to_pair_in.start()
+        to_sibling_in.start()
 
         def send(t, carry):
-            for n in range(2):
-                remote(h_ref.at[0, t], hb.at[1, 0, t], ys_sem.at[n], yr_sem.at[1, t], near[n]).start()
+            remote(h_ref.at[0, t], hb.at[0, 0, t], ys_sem.at[1], yr_sem.at[0, t], near[1]).start()
             return carry
         lax.fori_loop(0, cap, send, 0)
+
+        def send_near(t, carry):
+            remote(h_ref.at[0, t], hb.at[1, 0, t], ys_sem.at[0], yr_sem.at[1, t], near[0]).start()
+            return carry
+        lax.fori_loop(0, cap, send_near, 0)
 
     for s in range(2):
         for d in range(NX):
@@ -138,7 +167,7 @@
     into_smem.wait()
 
     def side(s):
-        return jnp.where(s == 0, yl, 1 - yl)
+        return jnp.where((s == 0) == outer, yl, 1 - yl)
 
     for s in range(2):
         for dz in range(NX):
@@ -172,18 +201,19 @@
 
     def multiply(s, t, carry):
         k = s * cap + t
-        held_x = far_x if s else near_x
+        held_x = second_x if s else first_x
 
         @pl.when(jnp.logical_and(lax.rem(k, CHUNK) == 0, k > 0))
         def _():
             send_chunk(k // CHUNK - 1)
 
-        if s:
-            @pl.when(t == 0)
-            def _():
-                to_pair.wait_recv()
-                forward_x.start()
-                forward_x.wait_recv()
+        crossed = forward_x if s else forward_x_in
+
+        @pl.when(jnp.logical_and(t == 0, outer if s else inner))
+        def _():
+            to_pair.wait_recv()
+            crossed.start()
+            crossed.wait_recv()
 
         pltpu.make_async_copy(h_ref.at[0, 0], hb.at[s, 2, t], rr_sem.at[2, k]).wait()
         for d in range(NX):
@@ -198,7 +228,7 @@
 
     def reach(i):
         free = i - 2 * LAG + 1
-        held = jnp.where(jnp.logical_and(inner, i < cap + 2 * LAG + 3), jnp.minimum(free, cap), free)
+        held = jnp.where(inner, jnp.minimum(free, 2 * (i - HOLD)), free)
         return jnp.clip(held, 0, total)
 
     def step(i, carry):
@@ -270,26 +300,32 @@
                 pltpu.make_async_copy(cb.at[0, 0, 0], out_ref.at[c, g, q], cr_sem.at[c, g, q]).wait()
 
 
-def combine(cap, bs, slabs, steps, meta, coeffs, potential, c_ref, prev_ref, dens_ref, next_ref, dout_ref, acc):
+def combine(cap, bs, slabs, steps, meta, coeffs, potential, c_ref, prev_ref, dens_ref, next_ref, dout_ref, even, odd):
     panel = pl.program_id(0)
     part = pl.program_id(1)
     columns = prev_ref.shape[0]
     width = prev_ref.shape[1]
+    spare = even.shape[1] // bs - 1
 
     @pl.when(part == 0)
     def _():
-        acc[...] = jnp.zeros_like(acc)
-        for g in range(2):
-            for q in range(NX):
-                for t in range(cap):
-                    row = pl.multiple_of(meta[panel, g, q, 1, t] * bs, bs)
+        even[...] = jnp.zeros_like(even)
+        odd[...] = jnp.zeros_like(odd)
+        for q in range(NX):
+            def add(t, carry):
+                for g, acc in ((0, even), (1, odd)):
+                    live = t < meta[panel, g, q, 2, 0]
+                    row = pl.multiple_of(jnp.where(live, meta[panel, g, q, 1, t], spare) * bs, bs)
                     acc[:, pl.ds(row, bs)] += c_ref[0, g, q, t].astype(jnp.float32)
+                return carry
+            lax.fori_loop(0, jnp.maximum(meta[panel, 0, q, 2, 0], meta[panel, 1, q, 2, 0]), add, 0)
 
     height = columns // slabs
     base = pl.multiple_of(part * width, width)
     for s in range(slabs):
         rows = pl.ds(s * height, height)
-        value = 2.0 * acc[rows, pl.ds(base, width)] - prev_ref[rows, :]
+        lanes = pl.ds(base, width)
+        value = 2.0 * (even[rows, lanes] + odd[rows, lanes]) - prev_ref[rows, :]
         next_ref[rows, :] = value
         dout_ref[rows, :] = dens_ref[rows, :] + coeffs[potential[s]] * value
 
@@ -300,11 +336,6 @@
     bs = h_tiles.shape[-1]
     slabs = potential.shape[0]
     panel_rows = local_rows // bs // 2
-    live = jnp.arange(cap, dtype=jnp.int32)[None, :] < tile_counts
-    rows = jnp.where(live, tile_rows, panel_rows)
-    lane_pad = ((0, 0), (0, 128 - cap))
-    meta = jnp.concatenate([jnp.pad(tile_cols, lane_pad), jnp.pad(rows, lane_pad),
-                            jnp.zeros((6, 128), jnp.int32)], axis=0)
     dma = pltpu.SemaphoreType.DMA
     bf16 = jnp.bfloat16
     anywhere = pl.BlockSpec(memory_space=pl.ANY)
@@ -315,13 +346,14 @@
             jax.ShapeDtypeStruct((2, 2, NX, cap, columns, bs), bf16),
             jax.ShapeDtypeStruct((2, 2, NX, 8, 128), jnp.int32),
         ),
-        in_specs=[anywhere, anywhere, pl.BlockSpec(memory_space=pltpu.VMEM)],
+        in_specs=[anywhere, anywhere] + [pl.BlockSpec(memory_space=pltpu.VMEM)] * 3,
         out_specs=(anywhere, anywhere),
         scratch_shapes=[
             pltpu.VMEM((2, local_rows // bs, columns, bs), bf16),
             pltpu.VMEM((2, local_rows // bs, columns, bs), bf16),
             pltpu.VMEM((2, NX, cap, bs, bs), bf16),
             pltpu.VMEM((2, NX, 2, cap, columns, bs), bf16),
+            pltpu.VMEM((8, 128), jnp.int32),
             pltpu.VMEM((2, NX, 8, 128), jnp.int32),
             pltpu.SMEM((2, NX, 8, 128), jnp.int32),
             dma((3,)), dma((3,)), dma,
@@ -336,7 +368,7 @@
         ),
         cost_estimate=pl.CostEstimate(flops=flops, bytes_accessed=16 * 1024 * 1024, transcendentals=0),
         name="exchange",
-    )(x_now, h_tiles, meta)
+    )(x_now, h_tiles, tile_cols, tile_rows, tile_counts)
     parts = 4
     width = local_rows // 2 // parts
     wide = pl.BlockSpec((columns, width), lambda p, i, *_: (0, p * parts + i))
@@ -354,7 +386,7 @@
                 wide, wide,
             ],
             out_specs=(wide, wide),
-            scratch_shapes=[pltpu.VMEM((columns, (panel_rows + 1) * bs), jnp.float32)],
+            scratch_shapes=[pltpu.VMEM((columns, (panel_rows + 1) * bs), jnp.float32)] * 2,
         ),
         compiler_params=pltpu.CompilerParams(vmem_limit_bytes=48 * 1024 * 1024),
         cost_estimate=pl.CostEstimate(flops=8 * columns * local_rows, bytes_accessed=24 * 1024 * 1024,

time: 169 us -> 153 us (0.905)
  Pallas kernels: 162 us -> 148 us
  other arithmetic: 2.4 us -> 0 us
    pallas_call x1, Pallas kernels: 148 us -> 135 us  [shards(): pl.pallas_call(functools.partial(exchange, cap, columns, bs), out_shape=(...]
where the time goes in v2:
time: 153 us; the launch traced here: 151 us
  Pallas kernels  148 us (97%)
    pallas_call x1, Pallas kernels, shards(): pl.pallas_call(functools.partial(exchange, cap, columns, bs), out_shape=(...  135 us
    pallas_call x1, Pallas kernels, shards(): pl.pallas_call(functools.partial(combine, cap, bs, slabs, parts), out_sha...  13.5 us

profile of v2, /device:TPU:13, one launch (start us, length us, event | category | flops | bytes accessed | tf_op | source)
XLA Modules:
  0.0 150.8 jit_solution(11166199574635218949)
XLA Ops:
  0.6 0.0 copy-start.3
  0.6 0.0 copy-start.2
  0.7 0.0 copy-start
  1.5 134.9 %exchange.1 = (bf16[2,2,4,12,64,256]{5,4,3,2,1,0:T(8,128)(2,1)}, s32[2,2,4,8,128]{4,3,2,1,0:T(8,128)}) custom-call(bf16[64,16384]{1,0:T(8,128)(2,1)} %x_ref.1, bf16[1,12,256,256]{3,2,1,0:T(8,128)(2,1)} %h_ref.1, s32[1,12]{1,0:T(1,128)} %cols_ref.1, s32[1,12]{1,0:T(1,128)} %rows_ref.1, s32[1,1]{1,0:T(1,128)S(6)} %copy.11.count_ref), custom_call_target="tpu_custom_call" | custom-call | flops 1610612736 | bytes 16777216 | tf_op jit(solution)/shard_map/exchange/pallas_call | solution.py:343
  136.4 0.0 copy-done.3
  136.4 0.0 copy-done.2
  136.4 0.0 copy-done
  136.4 0.0 copy-start.1
  136.4 0.8 copy-done.1
  137.3 13.5 %combine.1 = (f32[64,16384]{1,0:T(8,128)}, f32[64,16384]{1,0:T(8,128)}) custom-call(s32[2,2,4,8,128]{4,3,2,1,0:T(8,128)S(1)} %copy-done.1, f32[8]{0:T(128)S(1)} %copy-done.2, s32[4]{0:T(128)S(1)} %copy-done.3, bf16[2,2,4,12,64,256]{5,4,3,2,1,0:T(8,128)(2,1)} %get-tuple-element.5.c_ref, f32[64,16384]{1,0:T(8,128)S(1)} %copy-done, f32[64,16384]{1,0:T(8,128)} %dens_ref.1), custom_call_target="tpu_custom_call" | custom-call | flops 8388608 | bytes 25165824 | tf_op jit(solution)/shard_map/combine/pallas_call | solution.py:375
Async XLA Ops:
  0.6 135.8 %copy-start.3 = (s32[4]{0:T(128)S(1)}, s32[4]{0:T(128)}, u32[]{:S(2)}) copy-start(s32[4]{0:T(128)} %potential.1) | copy-start | bytes 52
  0.6 135.8 %copy-start.2 = (f32[8]{0:T(128)S(1)}, f32[8]{0:T(128)}, u32[]{:S(2)}) copy-start(f32[8]{0:T(128)} %coeffs.1) | copy-start | bytes 100
  0.7 135.8 %copy-start = (f32[64,16384]{1,0:T(8,128)S(1)}, f32[64,16384]{1,0:T(8,128)}, u32[]{:S(2)}) copy-start(f32[64,16384]{1,0:T(8,128)} %prev_ref.1) | copy-start | bytes 12582916
  136.4 0.8 copy-start.1

commit v3 on v2

--- a/solution.py
+++ b/solution.py
@@ -9,9 +9,12 @@
 
 MESH = pl.DeviceIdType.MESH
 NX = 4
-LAG = 4
-CHUNK = 1
-HOLD = 12
+LAG = 3
+LAG2 = 2
+HOLD = 9
+RATE = 3
+XL = 30
+FAR = 7
 
 
 def place():
@@ -138,11 +141,6 @@
         to_pair.start()
         to_sibling.start()
 
-        def send(t, carry):
-            remote(h_ref.at[0, t], hb.at[1, 0, t], ys_sem.at[0], yr_sem.at[1, t], far).start()
-            return carry
-        lax.fori_loop(0, cap, send, 0)
-
     @pl.when(inner)
     def _():
         to_pair_in.start()
@@ -182,41 +180,20 @@
                     pltpu.make_async_copy(mbuf.at[s, d], mout_ref.at[core, side(s), z],
                                           nr_sem.at[core, side(s), z]).start()
 
-    def send_chunk(q):
-        s = q // (cap // CHUNK)
-        first = lax.rem(q, cap // CHUNK) * CHUNK
-        slots = pl.ds(first, CHUNK)
-        for dz in range(NX):
-            z_to = wrap(z + dz)
-            d = wrap(z_to - x)
-            for dc in range(2):
-                c_to = other if dc else core
-                src = cb.at[s, d, c_to, slots]
-                dst = out_ref.at[core, side(s), z, slots]
-                arrived = cr_sem.at[core, side(s), z]
-                if dz or dc:
-                    remote(src, dst, cs_sem.at[s, dz, dc], arrived, device(x, y, z_to, c_to)).start()
-                else:
-                    pltpu.make_async_copy(src, dst, arrived).start()
-
-    def multiply(s, t, carry):
-        k = s * cap + t
+    def multiply(s, owners, t, carry):
         held_x = second_x if s else first_x
-
-        @pl.when(jnp.logical_and(lax.rem(k, CHUNK) == 0, k > 0))
-        def _():
-            send_chunk(k // CHUNK - 1)
-
-        crossed = forward_x if s else forward_x_in
-
-        @pl.when(jnp.logical_and(t == 0, outer if s else inner))
-        def _():
-            to_pair.wait_recv()
-            crossed.start()
-            crossed.wait_recv()
-
-        pltpu.make_async_copy(h_ref.at[0, 0], hb.at[s, 2, t], rr_sem.at[2, k]).wait()
-        for d in range(NX):
+        if owners == (0,):
+            crossed = forward_x if s else forward_x_in
+
+            @pl.when(jnp.logical_and(t == 0, outer if s else inner))
+            def _():
+                to_pair.wait_recv()
+                crossed.start()
+                crossed.wait_recv()
+
+        for d in owners:
+            if d == 2:
+                pltpu.make_async_copy(h_ref.at[0, 0], hb.at[s, d, t], rr_sem.at[d, s * cap + t]).wait()
             column = msm[s, d, 0, t]
             picked = jnp.concatenate([held_x[0, column], held_x[1, column]], axis=0)
             product = lax.dot_general(
@@ -226,12 +203,35 @@
             cb[s, d, 1, t] = product[slab:]
         return carry
 
-    def reach(i):
-        free = i - 2 * LAG + 1
-        held = jnp.where(inner, jnp.minimum(free, 2 * (i - HOLD)), free)
+    def deliver(s, owners, t, carry):
+        for d in owners:
+            z_to = wrap(x + d)
+            dst = out_ref.at[core, side(s), z, t]
+            arrived = cr_sem.at[core, side(s), z]
+            remote(cb.at[s, d, other, t], dst, cs_sem.at[s, d, 1], arrived, device(x, y, z_to, other)).start()
+
+            @pl.when(z_to != z)
+            def _(d=d, dst=dst, arrived=arrived, z_to=z_to):
+                remote(cb.at[s, d, core, t], dst, cs_sem.at[s, d, 0], arrived, device(x, y, z_to, core)).start()
+
+            @pl.when(z_to == z)
+            def _(d=d, dst=dst, arrived=arrived):
+                pltpu.make_async_copy(cb.at[s, d, core, t], dst, arrived).start()
+        return carry
+
+    kinds = (((0,), 0), ((1, 3), LAG), ((2,), LAG + LAG2))
+
+    def reach(i, lag):
+        free = i - lag + 1
+        held = jnp.where(inner, jnp.minimum(free, RATE * (i - HOLD)), free)
         return jnp.clip(held, 0, total)
 
     def step(i, carry):
+        @pl.when(jnp.logical_and(outer, jnp.logical_and(i >= FAR, i < FAR + cap)))
+        def _():
+            t = i - FAR
+            remote(h_ref.at[0, t], hb.at[1, 0, t], ys_sem.at[0], yr_sem.at[1, t], far).start()
+
         @pl.when(i < total)
         def _():
             s = i // cap
@@ -257,12 +257,15 @@
             def _():
                 remote(hb.at[s, 1, t], hb.at[s, 2, t], fs_sem.at[1, s], rr_sem.at[2, j], x_down).start()
 
-        done, until = reach(i - 1), reach(i)
-        lax.fori_loop(jnp.minimum(done, cap), jnp.minimum(until, cap), functools.partial(multiply, 0), 0)
-        lax.fori_loop(jnp.maximum(done - cap, 0), jnp.maximum(until - cap, 0), functools.partial(multiply, 1), 0)
+        for s in range(2):
+            for work in (multiply, deliver):
+                for owners, lag in kinds:
+                    done = jnp.clip(reach(i - 1, lag) - s * cap, 0, cap)
+                    until = jnp.clip(reach(i, lag) - s * cap, 0, cap)
+                    lax.fori_loop(done, until, functools.partial(work, s, owners), 0)
         return carry
 
-    lax.fori_loop(0, total + 2 * LAG, step, 0)
+    lax.fori_loop(0, total + LAG + LAG2, step, 0)
 
     to_sibling.wait_send()
     to_pair.wait_send()
@@ -273,7 +276,6 @@
     def _():
         pltpu.make_async_copy(h_ref.at[0], hb.at[0, 0], ys_sem.at[1]).wait()
 
-    send_chunk(jnp.int32(total // CHUNK - 1))
     for way in range(2):
         for s in range(2):
             pltpu.make_async_copy(h_ref.at[0], hb.at[s, 0], rs_sem.at[way, s]).wait()
@@ -292,7 +294,12 @@
             for dc in range(2):
                 if dz or dc:
                     pltpu.make_async_copy(mbuf.at[0, 0], mout_ref.at[0, 0, 0], ns_sem.at[s, dz, dc]).wait()
-                    pltpu.make_async_copy(cb.at[0, 0, 0], out_ref.at[0, 0, 0], cs_sem.at[s, dz, dc]).wait()
+        for d in range(NX):
+            pltpu.make_async_copy(cb.at[0, 0, 0], out_ref.at[0, 0, 0], cs_sem.at[s, d, 1]).wait()
+
+            @pl.when(wrap(x + d) != z)
+            def _(s=s, d=d):
+                pltpu.make_async_copy(cb.at[0, 0, 0], out_ref.at[0, 0, 0], cs_sem.at[s, d, 0]).wait()
     for c in range(2):
         for g in range(2):
             for q in range(NX):
@@ -346,7 +353,7 @@
             jax.ShapeDtypeStruct((2, 2, NX, cap, columns, bs), bf16),
             jax.ShapeDtypeStruct((2, 2, NX, 8, 128), jnp.int32),
         ),
-        in_specs=[anywhere, anywhere] + [pl.BlockSpec(memory_space=pltpu.VMEM)] * 3,
+        in_specs=[pl.BlockSpec(memory_space=pltpu.HBM)] * 2 + [pl.BlockSpec(memory_space=pltpu.VMEM)] * 3,
         out_specs=(anywhere, anywhere),
         scratch_shapes=[
             pltpu.VMEM((2, local_rows // bs, columns, bs), bf16),
@@ -364,12 +371,12 @@
             dma((2, NX, 2)), dma((2, 2, NX)), dma,
         ],
         compiler_params=pltpu.CompilerParams(
-            collective_id=0, has_side_effects=True, vmem_limit_bytes=56 * 1024 * 1024
+            collective_id=0, has_side_effects=True, vmem_limit_bytes=XL * 1024 * 1024
         ),
-        cost_estimate=pl.CostEstimate(flops=flops, bytes_accessed=16 * 1024 * 1024, transcendentals=0),
+        cost_estimate=pl.CostEstimate(flops=40 * flops, bytes_accessed=16 * 1024 * 1024, transcendentals=0),
         name="exchange",
-    )(x_now, h_tiles, tile_cols, tile_rows, tile_counts)
-    parts = 4
+    )(pltpu.with_memory_space_constraint(x_now, pltpu.HBM), pltpu.with_memory_space_constraint(h_tiles, pltpu.HBM), tile_cols, tile_rows, tile_counts)
+    parts = 2
     width = local_rows // 2 // parts
     wide = pl.BlockSpec((columns, width), lambda p, i, *_: (0, p * parts + i))
     return tuple(pl.pallas_call(
@@ -388,7 +395,7 @@
             out_specs=(wide, wide),
             scratch_shapes=[pltpu.VMEM((columns, (panel_rows + 1) * bs), jnp.float32)] * 2,
         ),
-        compiler_params=pltpu.CompilerParams(vmem_limit_bytes=48 * 1024 * 1024),
+        compiler_params=pltpu.CompilerParams(vmem_limit_bytes=30 * 1024 * 1024),
         cost_estimate=pl.CostEstimate(flops=8 * columns * local_rows, bytes_accessed=24 * 1024 * 1024,
                                       transcendentals=0),
         name="combine",

time: 153 us -> 143 us (0.935); the launches traced: 151 us -> 143 us
  Pallas kernels: 148 us -> 140 us
    pallas_call x1, Pallas kernels: 13.5 us -> 7.62 us  [shards(): pl.pallas_call(functools.partial(combine, cap, bs, slabs, parts), out_sha...]
    pallas_call x1, Pallas kernels: 135 us -> 133 us  [shards(): pl.pallas_call(functools.partial(exchange, cap, columns, bs), out_shape=(...]
where the time goes in v3:
time: 143 us
  Pallas kernels  140 us (98%)
    pallas_call x1, Pallas kernels, shards(): pl.pallas_call(functools.partial(exchange, cap, columns, bs), out_shape=(...  133 us
    pallas_call x1, Pallas kernels, shards(): pl.pallas_call(functools.partial(combine, cap, bs, slabs, parts), out_sha...  7.62 us

profile of v3, /device:TPU:13, one launch (start us, length us, event | category | flops | bytes accessed | tf_op | source)
XLA Modules:
  0.0 142.9 jit_solution(6330867829033480770)
XLA Ops:
  1.3 0.0 copy-start.4
  1.3 0.6 copy-done.4
  1.9 0.0 copy-start.5
  1.9 0.7 copy-done.5
  2.6 0.0 copy-start
  2.6 0.0 copy-start.1
  2.6 0.0 copy-start.2
  2.6 0.0 copy-start.3
  2.6 132.6 %exchange.1 = (bf16[2,2,4,12,64,256]{5,4,3,2,1,0:T(8,128)(2,1)S(1)}, s32[2,2,4,8,128]{4,3,2,1,0:T(8,128)S(1)}) custom-call(bf16[64,16384]{1,0:T(8,128)(2,1)} %x_ref.1, bf16[1,12,256,256]{3,2,1,0:T(8,128)(2,1)} %h_ref.1, s32[1,12]{1,0:T(1,128)S(1)} %copy-done.4, s32[1,12]{1,0:T(1,128)S(1)} %copy-done.5, s32[1,1]{1,0:T(1,128)S(6)} %copy.11.count_ref), custom_call_target="tpu_custom_call" | custom-call | flops 64424509440 | bytes 16777216 | tf_op jit(solution)/shard_map/exchange/pallas_call | solution.py:350
  135.3 0.0 copy-done
  135.3 0.0 copy-done.1
  135.3 0.0 copy-done.2
  135.3 0.0 copy-done.3
  135.3 7.6 %combine.1 = (f32[64,16384]{1,0:T(8,128)}, f32[64,16384]{1,0:T(8,128)}) custom-call(s32[2,2,4,8,128]{4,3,2,1,0:T(8,128)S(1)} %get-tuple-element.4.meta, f32[8]{0:T(128)S(1)} %copy-done.2, s32[4]{0:T(128)S(1)} %copy-done.3, bf16[2,2,4,12,64,256]{5,4,3,2,1,0:T(8,128)(2,1)S(1)} %get-tuple-element.5.c_ref, f32[64,16384]{1,0:T(8,128)S(1)} %copy-done, ...), custom_call_target="tpu_custom_call" | custom-call | flops 8388608 | bytes 25165824 | tf_op jit(solution)/shard_map/combine/pallas_call | solution.py:382
Async XLA Ops:
  1.3 0.7 copy-start.4
  1.9 0.7 copy-start.5
  2.6 132.7 %copy-start = (f32[64,16384]{1,0:T(8,128)S(1)}, f32[64,16384]{1,0:T(8,128)}, u32[]{:S(2)}) copy-start(f32[64,16384]{1,0:T(8,128)} %prev_ref.1) | copy-start | bytes 12582916
  2.6 132.7 %copy-start.1 = (f32[64,16384]{1,0:T(8,128)S(1)}, f32[64,16384]{1,0:T(8,128)}, u32[]{:S(2)}) copy-start(f32[64,16384]{1,0:T(8,128)} %dens_ref.1) | copy-start | bytes 12582916
  2.6 132.7 %copy-start.2 = (f32[8]{0:T(128)S(1)}, f32[8]{0:T(128)}, u32[]{:S(2)}) copy-start(f32[8]{0:T(128)} %coeffs.1) | copy-start | bytes 100
  2.6 132.7 %copy-start.3 = (s32[4]{0:T(128)S(1)}, s32[4]{0:T(128)}, u32[]{:S(2)}) copy-start(s32[4]{0:T(128)} %potential.1) | copy-start | bytes 52

commit v4 on v3

--- a/solution.py
+++ b/solution.py
@@ -11,10 +11,11 @@
 NX = 4
 LAG = 3
 LAG2 = 2
-HOLD = 9
+HOLD = 11
+HOLD_LOW = 7
 RATE = 3
 XL = 30
-FAR = 7
+FAR = 9
 
 
 def place():
@@ -36,7 +37,7 @@
     return lax.rem(value + 2 * NX, NX)
 
 
-def exchange(cap, slab, bs, x_ref, h_ref, cols_ref, rows_ref, count_ref, out_ref, mout_ref, first_x, second_x, hb, cb, m_own, mbuf, msm,
+def exchange(cap, slab, bs, x_ref, h_ref, cols_ref, rows_ref, count_ref, out_ref, mout_ref, first_lo, first_hi, second_lo, second_hi, hb, cb, m_own, mbuf, msm,
              xs_sem, xr_sem, xl_sem, ys_sem, yr_sem, rs_sem, rr_sem, fs_sem, cs_sem, cr_sem,
              ms_sem, mr_sem, ns_sem, nr_sem, sm_sem):
     x, yh, yl, z, core = place()
@@ -72,7 +73,9 @@
                 to = device(x, y, wrap(z + dz), other if dc else core)
                 pl.semaphore_signal(barrier, inc=1, device_id=to, device_id_type=MESH)
                 greeted += 1
-    blocks = first_x.shape[1]
+    blocks = first_lo.shape[1]
+    part = slab // 2
+    first, second = (first_lo, first_hi), (second_lo, second_hi)
     m_ref = m_own
     m_ref[...] = jnp.zeros(m_ref.shape, m_ref.dtype)
     m_ref[0:1, 0:cap] = cols_ref[...]
@@ -82,19 +85,21 @@
     def load_x(held):
         def one(b, carry):
             columns = pl.ds(pl.multiple_of(b * bs, bs), bs)
-            pltpu.make_async_copy(x_ref.at[:, columns], held.at[core, b], xl_sem).start()
+            for h in range(2):
+                rows = pl.ds(h * part, part)
+                pltpu.make_async_copy(x_ref.at[rows, columns], held[h].at[core, b], xl_sem.at[h]).start()
             return carry
         lax.fori_loop(0, blocks, one, 0)
 
     @pl.when(outer)
     def _():
-        load_x(first_x)
+        load_x(first)
 
     @pl.when(inner)
     def _():
-        load_x(second_x)
-
-    own_x = pltpu.make_async_copy(second_x.at[core], first_x.at[core], xl_sem)
+        load_x(second)
+
+    own_x = [pltpu.make_async_copy(second[h].at[core], first[h].at[core], xl_sem.at[h]) for h in range(2)]
 
     @pl.when(outer)
     def _():
@@ -122,29 +127,36 @@
             else:
                 remote(m_ref, mbuf.at[phase, d], ms_sem.at[half, d], mr_sem.at[phase, d], to).start()
 
-    own_x.wait()
+    for h in range(2):
+        own_x[h].wait()
+    pair_far = device(x, wrap(y_pair + 2), z, core)
     far = device(x, wrap(y + 2), z, core)
-    near = (pair, device(x, wrap(y_pair + 2), z, core))
-
-    def x_copies(own, other_x):
+    near = (pair, pair_far)
+
+    def x_copies(own, crossed):
         return (
-            remote(own.at[core], own.at[core], xs_sem.at[0], xr_sem.at[0], sibling),
-            remote(own.at[core], own.at[core], xs_sem.at[1], xr_sem.at[1], pair),
-            remote(other_x.at[core], other_x.at[core], xs_sem.at[2], xr_sem.at[2], sibling),
+            [remote(own[h].at[core], own[h].at[core], xs_sem.at[0, h], xr_sem.at[0, h], sibling) for h in range(2)],
+            [remote(own[h].at[core], own[h].at[core], xs_sem.at[1, h], xr_sem.at[1, h], pair) for h in range(2)],
+            [remote(crossed[h].at[core], crossed[h].at[core], xs_sem.at[2, h], xr_sem.at[2, h], sibling)
+             for h in range(2)],
         )
 
-    to_sibling, to_pair, forward_x = x_copies(first_x, second_x)
-    to_sibling_in, to_pair_in, forward_x_in = x_copies(second_x, first_x)
+    to_sibling, to_pair, forward_x = x_copies(first, second)
+    to_sibling_in, to_pair_in, forward_x_in = x_copies(second, first)
 
     @pl.when(outer)
     def _():
-        to_pair.start()
-        to_sibling.start()
+        for h in range(2):
+            to_pair[h].start()
+        for h in range(2):
+            to_sibling[h].start()
 
     @pl.when(inner)
     def _():
-        to_pair_in.start()
-        to_sibling_in.start()
+        for h in range(2):
+            to_pair_in[h].start()
+        for h in range(2):
+            to_sibling_in[h].start()
 
         def send(t, carry):
             remote(h_ref.at[0, t], hb.at[0, 0, t], ys_sem.at[1], yr_sem.at[0, t], near[1]).start()
@@ -161,7 +173,8 @@
             pltpu.make_async_copy(m_ref, mbuf.at[s, d], mr_sem.at[s, d]).wait()
     into_smem = pltpu.make_async_copy(mbuf, msm, sm_sem)
     into_smem.start()
-    to_sibling.wait_recv()
+    for h in range(2):
+        to_sibling[h].wait_recv()
     into_smem.wait()
 
     def side(s):
@@ -180,51 +193,68 @@
                     pltpu.make_async_copy(mbuf.at[s, d], mout_ref.at[core, side(s), z],
                                           nr_sem.at[core, side(s), z]).start()
 
-    def multiply(s, owners, t, carry):
-        held_x = second_x if s else first_x
+    whole, low, high = (0, 1), (0,), (1,)
+
+    def multiply(s, owners, halves, t, carry):
+        held = second if s else first
         if owners == (0,):
             crossed = forward_x if s else forward_x_in
 
             @pl.when(jnp.logical_and(t == 0, outer if s else inner))
             def _():
-                to_pair.wait_recv()
-                crossed.start()
-                crossed.wait_recv()
+                for h in halves:
+                    to_pair[h].wait_recv()
+                    crossed[h].start()
+                for h in halves:
+                    crossed[h].wait_recv()
 
         for d in owners:
-            if d == 2:
+            if d == 2 and halves != high:
                 pltpu.make_async_copy(h_ref.at[0, 0], hb.at[s, d, t], rr_sem.at[d, s * cap + t]).wait()
             column = msm[s, d, 0, t]
-            picked = jnp.concatenate([held_x[0, column], held_x[1, column]], axis=0)
+            picked = jnp.concatenate([held[h][c, column] for c in range(2) for h in halves], axis=0)
             product = lax.dot_general(
                 picked, hb[s, d, t], (((1,), (1,)), ((), ())), preferred_element_type=jnp.float32
             ).astype(jnp.bfloat16)
-            cb[s, d, 0, t] = product[:slab]
-            cb[s, d, 1, t] = product[slab:]
+            count = part * len(halves)
+            rows = pl.ds(halves[0] * part, count)
+            cb[s, d, 0, t, rows] = product[:count]
+            cb[s, d, 1, t, rows] = product[count:]
         return carry
 
-    def deliver(s, owners, t, carry):
+    def deliver(s, owners, halves, t, carry):
+        rows = pl.ds(halves[0] * part, part * len(halves))
         for d in owners:
             z_to = wrap(x + d)
-            dst = out_ref.at[core, side(s), z, t]
+            dst = out_ref.at[core, side(s), z, t, rows]
+            theirs, mine = cb.at[s, d, other, t, rows], cb.at[s, d, core, t, rows]
             arrived = cr_sem.at[core, side(s), z]
-            remote(cb.at[s, d, other, t], dst, cs_sem.at[s, d, 1], arrived, device(x, y, z_to, other)).start()
+            remote(theirs, dst, cs_sem.at[s, d, 1], arrived, device(x, y, z_to, other)).start()
 
             @pl.when(z_to != z)
-            def _(d=d, dst=dst, arrived=arrived, z_to=z_to):
-                remote(cb.at[s, d, core, t], dst, cs_sem.at[s, d, 0], arrived, device(x, y, z_to, core)).start()
+            def _(d=d, dst=dst, arrived=arrived, z_to=z_to, mine=mine):
+                remote(mine, dst, cs_sem.at[s, d, 0], arrived, device(x, y, z_to, core)).start()
 
             @pl.when(z_to == z)
-            def _(d=d, dst=dst, arrived=arrived):
-                pltpu.make_async_copy(cb.at[s, d, core, t], dst, arrived).start()
+            def _(dst=dst, arrived=arrived, mine=mine):
+                pltpu.make_async_copy(mine, dst, arrived).start()
         return carry
 
     kinds = (((0,), 0), ((1, 3), LAG), ((2,), LAG + LAG2))
 
-    def reach(i, lag):
+    def reach(i, lag, hold):
         free = i - lag + 1
-        held = jnp.where(inner, jnp.minimum(free, RATE * (i - HOLD)), free)
-        return jnp.clip(held, 0, total)
+        if hold is not None:
+            free = jnp.minimum(free, RATE * (i - hold))
+        return free
+
+    passes = ((0, whole, None, outer), (0, low, HOLD_LOW, inner), (0, high, HOLD, inner), (1, whole, None, None))
+
+    def span(i, s, lag, hold, who):
+        free = reach(i, lag, hold) if s == 0 else jnp.where(
+            outer, reach(i, lag, None), jnp.minimum(reach(i, lag, None), RATE * (i - HOLD)))
+        free = jnp.clip(free - s * cap, 0, cap)
+        return free if who is None else jnp.where(who, free, 0)
 
     def step(i, carry):
         @pl.when(jnp.logical_and(outer, jnp.logical_and(i >= FAR, i < FAR + cap)))
@@ -257,19 +287,19 @@
             def _():
                 remote(hb.at[s, 1, t], hb.at[s, 2, t], fs_sem.at[1, s], rr_sem.at[2, j], x_down).start()
 
-        for s in range(2):
+        for s, halves, hold, who in passes:
             for work in (multiply, deliver):
                 for owners, lag in kinds:
-                    done = jnp.clip(reach(i - 1, lag) - s * cap, 0, cap)
-                    until = jnp.clip(reach(i, lag) - s * cap, 0, cap)
-                    lax.fori_loop(done, until, functools.partial(work, s, owners), 0)
+                    done, until = span(i - 1, s, lag, hold, who), span(i, s, lag, hold, who)
+                    lax.fori_loop(done, until, functools.partial(work, s, owners, halves), 0)
         return carry
 
     lax.fori_loop(0, total + LAG + LAG2, step, 0)
 
-    to_sibling.wait_send()
-    to_pair.wait_send()
-    forward_x.wait_send()
+    for h in range(2):
+        to_sibling[h].wait_send()
+        to_pair[h].wait_send()
+        forward_x[h].wait_send()
     pltpu.make_async_copy(h_ref.at[0], hb.at[0, 0], ys_sem.at[0]).wait()
 
     @pl.when(inner)
@@ -356,14 +386,16 @@
         in_specs=[pl.BlockSpec(memory_space=pltpu.HBM)] * 2 + [pl.BlockSpec(memory_space=pltpu.VMEM)] * 3,
         out_specs=(anywhere, anywhere),
         scratch_shapes=[
-            pltpu.VMEM((2, local_rows // bs, columns, bs), bf16),
-            pltpu.VMEM((2, local_rows // bs, columns, bs), bf16),
+            pltpu.VMEM((2, local_rows // bs, columns // 2, bs), bf16),
+            pltpu.VMEM((2, local_rows // bs, columns // 2, bs), bf16),
+            pltpu.VMEM((2, local_rows // bs, columns // 2, bs), bf16),
+            pltpu.VMEM((2, local_rows // bs, columns // 2, bs), bf16),
             pltpu.VMEM((2, NX, cap, bs, bs), bf16),
             pltpu.VMEM((2, NX, 2, cap, columns, bs), bf16),
             pltpu.VMEM((8, 128), jnp.int32),
             pltpu.VMEM((2, NX, 8, 128), jnp.int32),
             pltpu.SMEM((2, NX, 8, 128), jnp.int32),
-            dma((3,)), dma((3,)), dma,
+            dma((3, 2)), dma((3, 2)), dma((2,)),
             dma((2,)), dma((2, cap)),
             dma((2, 2)), dma((4, 2 * cap)), dma((2, 2)),
             dma((2, NX, 2)), dma((2, 2, NX)),
@@ -376,7 +408,7 @@
         cost_estimate=pl.CostEstimate(flops=40 * flops, bytes_accessed=16 * 1024 * 1024, transcendentals=0),
         name="exchange",
     )(pltpu.with_memory_space_constraint(x_now, pltpu.HBM), pltpu.with_memory_space_constraint(h_tiles, pltpu.HBM), tile_cols, tile_rows, tile_counts)
-    parts = 2
+    parts = 1
     width = local_rows // 2 // parts
     wide = pl.BlockSpec((columns, width), lambda p, i, *_: (0, p * parts + i))
     return tuple(pl.pallas_call(

time: 143 us -> 138 us (0.965)
  Pallas kernels: 140 us -> 134 us
    pallas_call x1, Pallas kernels: 133 us -> 127 us  [shards(): pl.pallas_call(functools.partial(exchange, cap, columns, bs), out_shape=(...]
where the time goes in v4:
time: 138 us; the launch traced here: 137 us
  Pallas kernels  134 us (97%)
    pallas_call x1, Pallas kernels, shards(): pl.pallas_call(functools.partial(exchange, cap, columns, bs), out_shape=(...  127 us
    pallas_call x1, Pallas kernels, shards(): pl.pallas_call(functools.partial(combine, cap, bs, slabs, parts), out_sha...  7.11 us

profile of v4, /device:TPU:13, one launch (start us, length us, event | category | flops | bytes accessed | tf_op | source)
XLA Modules:
  0.0 136.8 jit_solution(11171568982356058568)
XLA Ops:
  1.3 0.0 copy-start.4
  1.3 0.6 copy-done.4
  1.9 0.0 copy-start.5
  1.9 0.7 copy-done.5
  2.6 0.0 copy-start
  2.6 0.0 copy-start.1
  2.6 0.0 copy-start.2
  2.6 0.0 copy-start.3
  2.6 127.0 %exchange.1 = (bf16[2,2,4,12,64,256]{5,4,3,2,1,0:T(8,128)(2,1)S(1)}, s32[2,2,4,8,128]{4,3,2,1,0:T(8,128)S(1)}) custom-call(bf16[64,16384]{1,0:T(8,128)(2,1)} %x_ref.1, bf16[1,12,256,256]{3,2,1,0:T(8,128)(2,1)} %h_ref.1, s32[1,12]{1,0:T(1,128)S(1)} %copy-done.4, s32[1,12]{1,0:T(1,128)S(1)} %copy-done.5, s32[1,1]{1,0:T(1,128)S(6)} %copy.11.count_ref), custom_call_target="tpu_custom_call" | custom-call | flops 64424509440 | bytes 16777216 | tf_op jit(solution)/shard_map/exchange/pallas_call | solution.py:380
  129.6 0.0 copy-done
  129.6 0.0 copy-done.1
  129.7 0.0 copy-done.2
  129.7 0.0 copy-done.3
  129.7 7.1 %combine.1 = (f32[64,16384]{1,0:T(8,128)}, f32[64,16384]{1,0:T(8,128)}) custom-call(s32[2,2,4,8,128]{4,3,2,1,0:T(8,128)S(1)} %get-tuple-element.4.meta, f32[8]{0:T(128)S(1)} %copy-done.2, s32[4]{0:T(128)S(1)} %copy-done.3, bf16[2,2,4,12,64,256]{5,4,3,2,1,0:T(8,128)(2,1)S(1)} %get-tuple-element.5.c_ref, f32[64,16384]{1,0:T(8,128)S(1)} %copy-done, ...), custom_call_target="tpu_custom_call" | custom-call | flops 8388608 | bytes 25165824 | tf_op jit(solution)/shard_map/combine/pallas_call | solution.py:414
Async XLA Ops:
  1.3 0.7 copy-start.4
  1.9 0.7 copy-start.5
  2.6 127.0 %copy-start = (f32[64,16384]{1,0:T(8,128)S(1)}, f32[64,16384]{1,0:T(8,128)}, u32[]{:S(2)}) copy-start(f32[64,16384]{1,0:T(8,128)} %prev_ref.1) | copy-start | bytes 12582916
  2.6 127.0 %copy-start.1 = (f32[64,16384]{1,0:T(8,128)S(1)}, f32[64,16384]{1,0:T(8,128)}, u32[]{:S(2)}) copy-start(f32[64,16384]{1,0:T(8,128)} %dens_ref.1) | copy-start | bytes 12582916
  2.6 127.1 %copy-start.2 = (f32[8]{0:T(128)S(1)}, f32[8]{0:T(128)}, u32[]{:S(2)}) copy-start(f32[8]{0:T(128)} %coeffs.1) | copy-start | bytes 100
  2.6 127.1 %copy-start.3 = (s32[4]{0:T(128)S(1)}, s32[4]{0:T(128)}, u32[]{:S(2)}) copy-start(s32[4]{0:T(128)} %potential.1) | copy-start | bytes 52

commit v5 on v4

--- a/solution.py
+++ b/solution.py
@@ -10,12 +10,13 @@
 MESH = pl.DeviceIdType.MESH
 NX = 4
 LAG = 3
-LAG2 = 2
-HOLD = 11
-HOLD_LOW = 7
+LAG2 = 3
+HOLD = 12
+HOLD_LOW = 8
 RATE = 3
 XL = 30
 FAR = 9
+EARLY = 2
 
 
 def place():
@@ -109,6 +110,8 @@
         lax.fori_loop(0, cap, load, 0)
 
     pl.semaphore_wait(barrier, greeted)
+    far = device(x, wrap(y + 2), z, core)
+    near = (pair, device(x, wrap(y_pair + 2), z, core))
 
     for d in range(NX):
         for half in range(2):
@@ -127,12 +130,15 @@
             else:
                 remote(m_ref, mbuf.at[phase, d], ms_sem.at[half, d], mr_sem.at[phase, d], to).start()
 
+    @pl.when(inner)
+    def _():
+        def send(t, carry):
+            remote(h_ref.at[0, t], hb.at[0, 0, t], ys_sem.at[1], yr_sem.at[0, t], near[1]).start()
+            return carry
+        lax.fori_loop(0, cap, send, 0)
+
     for h in range(2):
         own_x[h].wait()
-    pair_far = device(x, wrap(y_pair + 2), z, core)
-    far = device(x, wrap(y + 2), z, core)
-    near = (pair, pair_far)
-
     def x_copies(own, crossed):
         return (
             [remote(own[h].at[core], own[h].at[core], xs_sem.at[0, h], xr_sem.at[0, h], sibling) for h in range(2)],
@@ -158,40 +164,36 @@
         for h in range(2):
             to_sibling_in[h].start()
 
-        def send(t, carry):
-            remote(h_ref.at[0, t], hb.at[0, 0, t], ys_sem.at[1], yr_sem.at[0, t], near[1]).start()
-            return carry
-        lax.fori_loop(0, cap, send, 0)
-
         def send_near(t, carry):
             remote(h_ref.at[0, t], hb.at[1, 0, t], ys_sem.at[0], yr_sem.at[1, t], near[0]).start()
             return carry
         lax.fori_loop(0, cap, send_near, 0)
 
-    for s in range(2):
-        for d in range(NX):
-            pltpu.make_async_copy(m_ref, mbuf.at[s, d], mr_sem.at[s, d]).wait()
-    into_smem = pltpu.make_async_copy(mbuf, msm, sm_sem)
-    into_smem.start()
-    for h in range(2):
-        to_sibling[h].wait_recv()
-    into_smem.wait()
-
     def side(s):
         return jnp.where((s == 0) == outer, yl, 1 - yl)
 
-    for s in range(2):
-        for dz in range(NX):
-            z_to = wrap(z + dz)
-            d = wrap(z_to - x)
-            for dc in range(2):
-                if dz or dc:
-                    to = device(x, y, z_to, other if dc else core)
-                    remote(mbuf.at[s, d], mout_ref.at[core, side(s), z], ns_sem.at[s, dz, dc],
-                           nr_sem.at[core, side(s), z], to).start()
-                else:
-                    pltpu.make_async_copy(mbuf.at[s, d], mout_ref.at[core, side(s), z],
-                                          nr_sem.at[core, side(s), z]).start()
+    def positions():
+        for s in range(2):
+            for d in range(NX):
+                pltpu.make_async_copy(m_ref, mbuf.at[s, d], mr_sem.at[s, d]).wait()
+        into_smem = pltpu.make_async_copy(mbuf, msm, sm_sem)
+        into_smem.start()
+        for h in range(2):
+            to_sibling[h].wait_recv()
+        into_smem.wait()
+
+        for s in range(2):
+            for dz in range(NX):
+                z_to = wrap(z + dz)
+                d = wrap(z_to - x)
+                for dc in range(2):
+                    if dz or dc:
+                        to = device(x, y, z_to, other if dc else core)
+                        remote(mbuf.at[s, d], mout_ref.at[core, side(s), z], ns_sem.at[s, dz, dc],
+                               nr_sem.at[core, side(s), z], to).start()
+                    else:
+                        pltpu.make_async_copy(mbuf.at[s, d], mout_ref.at[core, side(s), z],
+                                              nr_sem.at[core, side(s), z]).start()
 
     whole, low, high = (0, 1), (0,), (1,)
 
@@ -240,7 +242,7 @@
                 pltpu.make_async_copy(mine, dst, arrived).start()
         return carry
 
-    kinds = (((0,), 0), ((1, 3), LAG), ((2,), LAG + LAG2))
+    kinds = (((0,), EARLY), ((1, 3), LAG), ((2,), LAG + LAG2))
 
     def reach(i, lag, hold):
         free = i - lag + 1
@@ -286,6 +288,10 @@
             @pl.when(lax.rem(j, 2) == 1)
             def _():
                 remote(hb.at[s, 1, t], hb.at[s, 2, t], fs_sem.at[1, s], rr_sem.at[2, j], x_down).start()
+
+        @pl.when(i == EARLY)
+        def _():
+            positions()
 
         for s, halves, hold, who in passes:
             for work in (multiply, deliver):
@@ -407,7 +413,8 @@
         ),
         cost_estimate=pl.CostEstimate(flops=40 * flops, bytes_accessed=16 * 1024 * 1024, transcendentals=0),
         name="exchange",
-    )(pltpu.with_memory_space_constraint(x_now, pltpu.HBM), pltpu.with_memory_space_constraint(h_tiles, pltpu.HBM), tile_cols, tile_rows, tile_counts)
+    )(pltpu.with_memory_space_constraint(x_now, pltpu.HBM), pltpu.with_memory_space_constraint(h_tiles, pltpu.HBM),
+      pltpu.with_memory_space_constraint(tile_cols, pltpu.HBM), pltpu.with_memory_space_constraint(tile_rows, pltpu.HBM), tile_counts)
     parts = 1
     width = local_rows // 2 // parts
     wide = pl.BlockSpec((columns, width), lambda p, i, *_: (0, p * parts + i))

time: 138 us -> 136 us (0.986)
  no operation moved by 1% of the time
where the time goes in v5:
time: 136 us; the launch traced here: 135 us
  Pallas kernels  134 us (99%)
    pallas_call x1, Pallas kernels, shards(): pl.pallas_call(functools.partial(exchange, cap, columns, bs), out_shape=(...  127 us
    pallas_call x1, Pallas kernels, shards(): pl.pallas_call(functools.partial(combine, cap, bs, slabs, parts), out_sha...  7.43 us

profile of v5, /device:TPU:13, one launch (start us, length us, event | category | flops | bytes accessed | tf_op | source)
XLA Modules:
  0.0 135.4 jit_solution(17836133688467664061)
XLA Ops:
  1.3 0.0 copy-start
  1.3 0.0 copy-start.1
  1.3 0.0 copy-start.2
  1.3 0.0 copy-start.3
  1.3 126.6 %exchange.1 = (bf16[2,2,4,12,64,256]{5,4,3,2,1,0:T(8,128)(2,1)S(1)}, s32[2,2,4,8,128]{4,3,2,1,0:T(8,128)S(1)}) custom-call(bf16[64,16384]{1,0:T(8,128)(2,1)} %x_ref.1, bf16[1,12,256,256]{3,2,1,0:T(8,128)(2,1)} %h_ref.1, s32[1,12]{1,0:T(1,128)} %cols_ref.1, s32[1,12]{1,0:T(1,128)} %rows_ref.1, s32[1,1]{1,0:T(1,128)S(6)} %copy.11.count_ref), custom_call_target="tpu_custom_call" | custom-call | flops 64424509440 | bytes 16777216 | tf_op jit(solution)/shard_map/exchange/pallas_call | solution.py:386
  127.9 0.0 copy-done
  127.9 0.0 copy-done.1
  127.9 0.0 copy-done.2
  127.9 0.0 copy-done.3
  127.9 7.4 %combine.1 = (f32[64,16384]{1,0:T(8,128)}, f32[64,16384]{1,0:T(8,128)}) custom-call(s32[2,2,4,8,128]{4,3,2,1,0:T(8,128)S(1)} %get-tuple-element.4.meta, f32[8]{0:T(128)S(1)} %copy-done.2, s32[4]{0:T(128)S(1)} %copy-done.3, bf16[2,2,4,12,64,256]{5,4,3,2,1,0:T(8,128)(2,1)S(1)} %get-tuple-element.5.c_ref, f32[64,16384]{1,0:T(8,128)S(1)} %copy-done, ...), custom_call_target="tpu_custom_call" | custom-call | flops 8388608 | bytes 25165824 | tf_op jit(solution)/shard_map/combine/pallas_call | solution.py:421
Async XLA Ops:
  1.3 126.6 %copy-start = (f32[64,16384]{1,0:T(8,128)S(1)}, f32[64,16384]{1,0:T(8,128)}, u32[]{:S(2)}) copy-start(f32[64,16384]{1,0:T(8,128)} %prev_ref.1) | copy-start | bytes 12582916
  1.3 126.6 %copy-start.1 = (f32[64,16384]{1,0:T(8,128)S(1)}, f32[64,16384]{1,0:T(8,128)}, u32[]{:S(2)}) copy-start(f32[64,16384]{1,0:T(8,128)} %dens_ref.1) | copy-start | bytes 12582916
  1.3 126.6 %copy-start.2 = (f32[8]{0:T(128)S(1)}, f32[8]{0:T(128)}, u32[]{:S(2)}) copy-start(f32[8]{0:T(128)} %coeffs.1) | copy-start | bytes 100
  1.3 126.6 %copy-start.3 = (s32[4]{0:T(128)S(1)}, s32[4]{0:T(128)}, u32[]{:S(2)}) copy-start(s32[4]{0:T(128)} %potential.1) | copy-start | bytes 52
